TPU v7x, 512 devices: a whole 4x4x16 slice. The times are simulated.
512 devices in a mesh: src: 64 (over z, y), ccd: 8 (over x, core).
Axes of the slice: x: 4, y: 4, z: 16, core: 2. Of those that a mesh axis runs over, the one named last changes fastest.
Arguments:
- design: float32 [5, 4194304], P(None, ('src', 'ccd')), may hold values from -6 to 6
- observed: float32 [4194304], P(('src', 'ccd')), may hold values from -12 to 12
- weight: float32 [4194304], P(('src', 'ccd')), may hold values from 0.25 to 4
- phase_frac: float32 [4194304], P(('src', 'ccd')), may hold values from 0 to 1
- axis_factors: float32 [3, 4194304], P(None, ('src', 'ccd')), may hold values from -6 to 6
- source_index: int32 [4194304], P(('src', 'ccd')), may hold values from 0 to 1023
- knot_index: int32 [4194304], P(('src', 'ccd')), may hold values from 0 to 127
- counts: int32 [64, 8, 64], P('src', 'ccd'), may hold values from 1 to 128, as said below
Outputs:
- source_params: float32 [5, 65536], P(None, 'src')
- attitude: float32 [3, 8192], P(None, 'src')
- residual: float32 [4194304], P(('src', 'ccd'))
Inputs may be any that keep to these rules, and one draw needn't show every extreme that they name: Slot l of device (p, c) is live when l % 128 < counts[p, c, l // 128]; every device has one full block of 128 live slots, and one time shard receives full blocks from every device.
All inputs are finite; a program needn't handle non-finite values.
Results may differ from a plain program's by a relative error of at most 0.0003.
Values sent between devices are 32-bit elements; how exact they have to be, the bound alone decides.
A program may use at most 64 MiB of HBM per device.

v0:
```python
import math

import jax
import jax.numpy as jnp
from jax import lax
from jax.sharding import PartitionSpec as P

SRC_DEV = 1024
KNOT_DEV = 128
ITERS = 3


src_ridge = 1.0
att_ridge = 1.0
relax_step = 0.15


def sent_to_all(array, axis):
    copies = jnp.broadcast_to(array, (lax.axis_size(axis), *array.shape))
    return lax.all_to_all(copies, axis, split_axis=0, concat_axis=0, tiled=True)


def taken_together(array, axis):
    everything = sent_to_all(array, axis)
    return jnp.sum(everything, axis=0)


def passed_along(block, axis, distance):
    devices = range(lax.axis_size(axis))
    route = [(i - distance, i) for i in devices if i - distance in devices]
    return lax.ppermute(block, axis, route)


def in_blocks(array, dim, length):
    before, after = (array.shape[:dim], array.shape[dim + 1 :])
    return jnp.moveaxis(array.reshape(*before, length, -1, *after), dim, 0)


def sent_and_summed(array, axis, dim):
    tiles = in_blocks(array, dim, lax.axis_size(axis))
    arrived = lax.all_to_all(tiles, axis, split_axis=0, concat_axis=0, tiled=True)
    return arrived.sum(axis=0)


def joined_along(tiles, dim):
    tiles = jnp.moveaxis(tiles, 0, dim)
    shape = tiles.shape
    return tiles.reshape(*shape[:dim], shape[dim] * shape[dim + 1], *shape[dim + 2 :])


def gather_directly(array, axis, dim):
    return joined_along(sent_to_all(array, axis), dim)


def row_moments(design_rows, observed_rows, weight_rows):
    products = []
    for m in range(5):
        for n in range(m, 5):
            products.append(design_rows[m] * design_rows[n] * weight_rows)
    for m in range(5):
        products.append(design_rows[m] * weight_rows * observed_rows)
    return jnp.stack(products)


def solve_small(moments):
    matrix = {}
    position = 0
    for m in range(5):
        for n in range(m, 5):
            matrix[m, n] = moments[position] + (src_ridge if m == n else 0.0)
            position += 1
    factor = {}
    for j in range(5):
        for i in range(j, 5):
            running = matrix[j, i]
            for k in range(j):
                running = running - factor[i, k] * factor[j, k]
            if i == j:
                factor[j, j] = jnp.sqrt(running)
            else:
                factor[i, j] = running / factor[j, j]
    forward = []
    for i in range(5):
        running = moments[15 + i]
        for k in range(i):
            running = running - factor[i, k] * forward[k]
        forward.append(running / factor[i, i])
    solution = [None] * 5
    for i in reversed(range(5)):
        running = forward[i]
        for k in range(i + 1, 5):
            running = running - factor[k, i] * solution[k]
        solution[i] = running / factor[i, i]
    return jnp.stack(solution)


def spline_basis(phase_rows):
    remain = 1.0 - phase_rows
    square = phase_rows * phase_rows
    cube_term = square * phase_rows
    return [
        remain * remain * remain / 6.0,
        (3.0 * cube_term - 6.0 * square + 4.0) / 6.0,
        (-3.0 * cube_term + 3.0 * square + 3.0 * phase_rows + 1.0) / 6.0,
        cube_term / 6.0,
    ]


def spread_groups(row_values, spline_terms, knot_rows, knot_count, groups):
    row_count = knot_rows.shape[0]
    group_rows = row_count // groups
    per_step = math.gcd(groups, max(1, 2048 // group_rows))
    step_count = groups // per_step
    stacked = jnp.concatenate([row_values * factor_row for factor_row in spline_terms], 0)
    blocked = stacked.reshape(12, step_count, per_step, group_rows).transpose(1, 2, 0, 3)
    knot_blocks = knot_rows.reshape(step_count, per_step, group_rows)
    columns = lax.iota(jnp.int32, knot_count)

    def add_block(carried, scan_items):
        values_blk, knots_blk = scan_items
        onehot = (knots_blk[:, :, None] == columns[None, None, :]).astype(jnp.float32)
        return (
            carried,
            jnp.einsum("gcr,grk->gck", values_blk, onehot, precision=lax.Precision.HIGHEST),
        )

    _, knot_sums = lax.scan(add_block, jnp.zeros((), jnp.int32), (blocked, knot_blocks))
    knot_sums = knot_sums.reshape(groups, 12, knot_count)
    return sum(
        (jnp.pad(knot_sums[:, 3 * j : 3 * j + 3], ((0, 0), (0, 0), (j, 3 - j))) for j in range(4))
    )


def predict_groups(extended_all, spline_terms, axis_rows, knot_rows, knot_count):
    groups = extended_all.shape[0]
    row_count = knot_rows.shape[0]
    group_rows = row_count // groups
    per_step = math.gcd(groups, max(1, 2048 // group_rows))
    step_count = groups // per_step
    windows = jnp.concatenate([extended_all[:, :, j : j + knot_count] for j in range(4)], 1)
    windows = windows.reshape(step_count, per_step, 12, knot_count)
    knot_blocks = knot_rows.reshape(step_count, per_step, group_rows)
    columns = lax.iota(jnp.int32, knot_count)

    def pick_block(carried, scan_items):
        windows_blk, knots_blk = scan_items
        onehot = (knots_blk[:, :, None] == columns[None, None, :]).astype(jnp.float32)
        return (
            carried,
            jnp.einsum("gck,grk->gcr", windows_blk, onehot, precision=lax.Precision.HIGHEST),
        )

    _, picked = lax.scan(pick_block, jnp.zeros((), jnp.int32), (windows, knot_blocks))
    picked = picked.transpose(2, 0, 1, 3).reshape(12, row_count)
    running = jnp.zeros_like(spline_terms[0])
    for j in range(4):
        running = running + spline_terms[j] * jnp.sum(axis_rows * picked[3 * j : 3 * j + 3], 0)
    return running


def knot_assemble(partial_sums):
    summed = taken_together(partial_sums, "ccd")
    spill_cols = passed_along(summed[:, -3:], "src", 1)
    return summed[:, :-3] + jnp.pad(spill_cols, ((0, 0), (0, summed.shape[1] - 6)))


def extend_edge(coefficients):
    edge_cols = passed_along(coefficients[:, :3], "src", -1)
    return jnp.concatenate([coefficients, edge_cols], 1)


def own_shard_sums(group_sums):
    return sent_and_summed(group_sums, "src", 0)[0]


def gather_extended(coefficients):
    return gather_directly(extend_edge(coefficients)[None], "src", 0)


def on_device(design, observed, weight, phase_frac, axis_factors, source_index, knot_index, counts):
    row_count = observed.shape[0]
    shards = lax.axis_size("src")
    cap_rows = row_count // shards
    knot_count = KNOT_DEV
    local_row = lax.iota(jnp.int32, row_count)
    slot_pos = (local_row % cap_rows).reshape(shards, cap_rows)
    live_mask = (slot_pos < counts[0, 0][:, None]).astype(jnp.float32).reshape(row_count)
    weight_live = weight * live_mask
    moments = jax.ops.segment_sum(
        row_moments(design, observed, weight_live).T, source_index, num_segments=SRC_DEV
    ).T
    params = solve_small(taken_together(moments, "ccd"))
    fitted = jnp.sum(design * jnp.take(params, source_index, axis=1), 0)
    params, resid_rows = (params, live_mask * (observed - fitted))
    spline_own = spline_basis(phase_frac)
    rhs_groups = spread_groups(
        weight_live * axis_factors * resid_rows, spline_own, knot_index, knot_count, shards
    )
    diag_groups = spread_groups(
        weight_live * axis_factors * axis_factors,
        [t * t for t in spline_own],
        knot_index,
        knot_count,
        shards,
    )
    totals = knot_assemble(own_shard_sums(jnp.concatenate([rhs_groups, diag_groups], 1)))
    rhs_knots = totals[:3]
    diag_knots = att_ridge + totals[3:]
    coefficients = relax_step * rhs_knots / diag_knots
    for iteration in range(1, ITERS):
        predicted = predict_groups(
            gather_extended(coefficients), spline_own, axis_factors, knot_index, knot_count
        )
        back_groups = spread_groups(
            weight_live * axis_factors * predicted, spline_own, knot_index, knot_count, shards
        )
        back_sums = knot_assemble(own_shard_sums(back_groups))
        normal_prod = att_ridge * coefficients + back_sums
        coefficients = coefficients + relax_step * (rhs_knots - normal_prod) / diag_knots
    predicted = predict_groups(
        gather_extended(coefficients), spline_own, axis_factors, knot_index, knot_count
    )
    residual = live_mask * (resid_rows - predicted)
    return (params, coefficients, residual)


def solution(mesh):
    in_specs = (
        P(None, ("src", "ccd")),
        P(("src", "ccd")),
        P(("src", "ccd")),
        P(("src", "ccd")),
        P(None, ("src", "ccd")),
        P(("src", "ccd")),
        P(("src", "ccd")),
        P("src", "ccd", None),
    )
    out_specs = (P(None, "src"), P(None, "src"), P(("src", "ccd")))
    return jax.shard_map(
        on_device, mesh=mesh, in_specs=in_specs, out_specs=out_specs, check_vma=False
    )
```

profile of v0, /device:TPU:1, one launch (start us, length us, event | category | flops | bytes accessed | tf_op | source)
XLA Modules:
  0.0 374.8 jit_solution(15477003784162670017)
XLA Ops:
  0.6 1.9 fusion.97
  5.2 2.6 copy.72
  7.9 44.4 %scatter_custom_fusion = f32[1024,20]{1,0:T(8,128)S(1)} fusion(s32[8192]{0:T(1024)S(1)} %copy-done.5, f32[8192,20]{1,0:T(8,128)} %copy.72, f32[]{:T(128)} %constant.104.clone.1), kind=kCustom, calls=%fused_computation.68 | custom fusion | flops 163840 | bytes 82432 | tf_op jit(solution)/shard_map/scatter-add | solution.py:189
  52.5 1.0 broadcast_in_dim.66
  53.5 10.3 %all-to-all-start = ((f32[8,20,1024]{2,1,0:T(8,128)}), f32[8,20,1024]{2,1,0:T(8,128)S(1)}, u32[]{:S(2)}, u32[]{:S(2)}) async-start(f32[8,20,1024]{2,1,0:T(8,128)} %broadcast_in_dim.66), calls=%async_computation | async-start | bytes 1572864 | tf_op jit(solution)/shard_map/all_to_all | solution.py:20
  63.8 2.6 copy.76
  66.5 9.5 %all-to-all-done = f32[8,20,1024]{2,1,0:T(8,128)S(1)} async-done(((f32[8,20,1024]{2,1,0:T(8,128)}), f32[8,20,1024]{2,1,0:T(8,128)S(1)}, u32[]{:S(2)}, u32[]{:S(2)}) %all-to-all-start) | async-done | bytes 655392 | tf_op jit(solution)/shard_map/all_to_all | solution.py:20
  76.7 27.7 %gather_fusion = f32[8192,5]{1,0:T(8,128)} fusion(f32[5,1024]{0,1:T(8,128)S(1)} %copy.75, s32[8192]{0:T(1024)S(1)} %fusion.39), kind=kCustom, calls=%fused_computation | custom fusion | bytes 360448 | tf_op jit(solution)/shard_map/jit(_take)/gather | solution.py:193
  104.4 5.2 %fusion.24 = f32[8192]{0:T(1024)S(1)} fusion(f32[5,8192]{0,1:T(8,128)} %copy.76, f32[8192,5]{1,0:T(8,128)} %gather_fusion, pred[8192]{0:T(1024)(128)(4,1)S(1)} %compare_and_fusion), kind=kLoop, calls=%fused_computation.59 | loop fusion | flops 114688 | bytes 368640 | tf_op jit(solution)/shard_map/reduce_sum | solution.py:193
  110.5 4.1 %while.77 = (s32[]{:T(128)}, f32[4,16,12,128]{3,1,0,2:T(8,128)S(1)}, f32[4,16,12,128]{3,1,0,2:T(8,128)S(1)}, s32[4,16,128]{2,1,0:T(8,128)S(1)}, s32[]{:T(128)}) while((s32[]{:T(128)}, f32[4,16,12,128]{3,1,0,2:T(8,128)S(1)}, f32[4,16,12,128]{3,1,0,2:T(8,128)S(1)}, s32[4,16,128]{2,1,0:T(8,128)S(1)}, s32[]{:T(128)}) %tuple.282), condition=%wide.region_4.5_spmd.clone, body=%wide.region_3.4_spmd.clone.sunk | while | flops 38010880 | bytes 647241 | solution.py:127
  114.8 4.1 %while.78 = (s32[]{:T(128)}, f32[4,16,12,128]{3,1,0,2:T(8,128)S(1)}, f32[4,16,12,128]{3,1,0,2:T(8,128)S(1)}, s32[4,16,128]{2,1,0:T(8,128)S(1)}, s32[]{:T(128)}) while((s32[]{:T(128)}, f32[4,16,12,128]{3,1,0,2:T(8,128)S(1)}, f32[4,16,12,128]{3,1,0,2:T(8,128)S(1)}, s32[4,16,128]{2,1,0:T(8,128)S(1)}, s32[]{:T(128)}) %tuple.283), condition=%wide.region_6.7_spmd.clone, body=%wide.region_5.6_spmd.clone.sunk | while | flops 38010880 | bytes 647241 | solution.py:127
  119.9 38.6 %all_to_all.51 = f32[64,1,6,131]{3,1,2,0:T(1,128)S(1)} all-to-all(f32[64,1,6,131]{3,1,2,0:T(1,128)S(1)} %copy.81), channel_id=1, replica_groups=mesh['src'=64,'ccd'=8] {'src'}, dimensions={0} | all-to-all | bytes 402432 | tf_op jit(solution)/shard_map/all_to_all | solution.py:41
  159.0 10.7 %all_to_all.52 = f32[8,1,786]{2,1,0:T(1,128)S(1)} all-to-all(f32[8,1,786]{2,1,0:T(1,128)S(1)} %reshape.168), channel_id=1, replica_groups=mesh['src'=64,'ccd'=8] {'ccd'}, dimensions={0} | all-to-all | bytes 50304 | tf_op jit(solution)/shard_map/all_to_all | solution.py:20
  171.1 2.7 collective-permute-start
  174.6 1.3 collective-permute-start.1
  175.9 3.3 collective-permute-done.1
  179.9 10.7 %all-to-all-start.3 = ((f32[64,1,3,131]{3,1,2,0:T(1,128)}), f32[64,1,3,131]{3,1,2,0:T(1,128)S(1)}, u32[]{:S(2)}, u32[]{:S(2)}) async-start(f32[64,1,3,131]{3,1,2,0:T(1,128)} %broadcast_in_dim.108), calls=%async_computation.3 | async-start | bytes 393216 | tf_op jit(solution)/shard_map/all_to_all | solution.py:20
  190.7 16.1 %all-to-all-done.3 = f32[64,1,3,131]{3,1,2,0:T(1,128)S(1)} async-done(((f32[64,1,3,131]{3,1,2,0:T(1,128)}), f32[64,1,3,131]{3,1,2,0:T(1,128)S(1)}, u32[]{:S(2)}, u32[]{:S(2)}) %all-to-all-start.3) | async-done | bytes 100640 | tf_op jit(solution)/shard_map/all_to_all | solution.py:20
  207.0 5.0 %while.79 = (s32[]{:T(128)}, f32[4,16,12,128]{3,2,1,0:T(8,128)S(1)}, f32[4,16,12,128]{3,1,0,2:T(8,128)S(1)}, s32[4,16,128]{2,1,0:T(8,128)S(1)}, s32[]{:T(128)}) while((s32[]{:T(128)}, f32[4,16,12,128]{3,2,1,0:T(8,128)S(1)}, f32[4,16,12,128]{3,1,0,2:T(8,128)S(1)}, s32[4,16,128]{2,1,0:T(8,128)S(1)}, s32[]{:T(128)}) %tuple.280), condition=%wide.region_10.11_spmd.clone, body=%wide.region_9.10_spmd.clone.sunk | while | flops 38010880 | bytes 450633 | solution.py:153
  207.1 1.2 fusion.104
  208.3 1.2 fusion.104
  209.6 1.2 fusion.104
  210.8 1.2 fusion.104
  213.0 4.1 %while.80 = (s32[]{:T(128)}, f32[4,16,12,128]{3,1,0,2:T(8,128)S(1)}, f32[4,16,12,128]{3,1,0,2:T(8,128)S(1)}, s32[4,16,128]{2,1,0:T(8,128)S(1)}, s32[]{:T(128)}) while((s32[]{:T(128)}, f32[4,16,12,128]{3,1,0,2:T(8,128)S(1)}, f32[4,16,12,128]{3,1,0,2:T(8,128)S(1)}, s32[4,16,128]{2,1,0:T(8,128)S(1)}, s32[]{:T(128)}) %tuple.284), condition=%wide.region_16.17_spmd.clone, body=%wide.region_15.16_spmd.clone.sunk | while | flops 38010880 | bytes 647241 | solution.py:127
  217.6 22.2 %all_to_all.53 = f32[64,1,3,131]{3,1,2,0:T(1,128)S(1)} all-to-all(f32[64,1,3,131]{3,1,2,0:T(1,128)S(1)} %copy.87), channel_id=1, replica_groups=mesh['src'=64,'ccd'=8] {'src'}, dimensions={0} | all-to-all | bytes 201216 | tf_op jit(solution)/shard_map/all_to_all | solution.py:41
  240.1 11.8 %all_to_all.54 = f32[8,1,393]{2,1,0:T(1,128)S(1)} all-to-all(f32[8,1,393]{2,1,0:T(1,128)S(1)} %reshape.170), channel_id=1, replica_groups=mesh['src'=64,'ccd'=8] {'ccd'}, dimensions={0} | all-to-all | bytes 25152 | tf_op jit(solution)/shard_map/all_to_all | solution.py:20
  252.7 2.1 collective-permute-start.2
  255.5 1.3 collective-permute-start.3
  256.8 3.3 collective-permute-done.3
  260.9 10.9 %all-to-all-start.6 = ((f32[64,1,3,131]{3,1,2,0:T(1,128)}), f32[64,1,3,131]{3,1,2,0:T(1,128)S(1)}, u32[]{:S(2)}, u32[]{:S(2)}) async-start(f32[64,1,3,131]{3,1,2,0:T(1,128)} %broadcast_in_dim.110), calls=%async_computation.6 | async-start | bytes 393216 | tf_op jit(solution)/shard_map/all_to_all | solution.py:20
  271.7 16.3 %all-to-all-done.6 = f32[64,1,3,131]{3,1,2,0:T(1,128)S(1)} async-done(((f32[64,1,3,131]{3,1,2,0:T(1,128)}), f32[64,1,3,131]{3,1,2,0:T(1,128)S(1)}, u32[]{:S(2)}, u32[]{:S(2)}) %all-to-all-start.6) | async-done | bytes 100640 | tf_op jit(solution)/shard_map/all_to_all | solution.py:20
  288.3 5.0 %while.81 = (s32[]{:T(128)}, f32[4,16,12,128]{3,2,1,0:T(8,128)S(1)}, f32[4,16,12,128]{3,1,0,2:T(8,128)S(1)}, s32[4,16,128]{2,1,0:T(8,128)S(1)}, s32[]{:T(128)}) while((s32[]{:T(128)}, f32[4,16,12,128]{3,2,1,0:T(8,128)S(1)}, f32[4,16,12,128]{3,1,0,2:T(8,128)S(1)}, s32[4,16,128]{2,1,0:T(8,128)S(1)}, s32[]{:T(128)}) %tuple.281), condition=%wide.region_20.21_spmd.clone, body=%wide.region_19.20_spmd.clone.sunk | while | flops 38010880 | bytes 450633 | solution.py:153
  288.3 1.2 fusion.105
  289.6 1.2 fusion.105
  290.8 1.2 fusion.105
  292.1 1.2 fusion.105
  294.3 4.1 %while.82 = (s32[]{:T(128)}, f32[4,16,12,128]{3,1,0,2:T(8,128)S(1)}, f32[4,16,12,128]{3,1,0,2:T(8,128)S(1)}, s32[4,16,128]{2,1,0:T(8,128)S(1)}, s32[]{:T(128)}) while((s32[]{:T(128)}, f32[4,16,12,128]{3,1,0,2:T(8,128)S(1)}, f32[4,16,12,128]{3,1,0,2:T(8,128)S(1)}, s32[4,16,128]{2,1,0:T(8,128)S(1)}, s32[]{:T(128)}) %tuple.285), condition=%wide.region_26.27_spmd.clone, body=%wide.region_25.26_spmd.clone.sunk | while | flops 38010880 | bytes 647241 | solution.py:127
  298.9 22.2 %all_to_all.55 = f32[64,1,3,131]{3,1,2,0:T(1,128)S(1)} all-to-all(f32[64,1,3,131]{3,1,2,0:T(1,128)S(1)} %copy.93), channel_id=1, replica_groups=mesh['src'=64,'ccd'=8] {'src'}, dimensions={0} | all-to-all | bytes 201216 | tf_op jit(solution)/shard_map/all_to_all | solution.py:41
  321.3 11.8 %all_to_all.56 = f32[8,1,393]{2,1,0:T(1,128)S(1)} all-to-all(f32[8,1,393]{2,1,0:T(1,128)S(1)} %reshape.172), channel_id=1, replica_groups=mesh['src'=64,'ccd'=8] {'ccd'}, dimensions={0} | all-to-all | bytes 25152 | tf_op jit(solution)/shard_map/all_to_all | solution.py:20
  334.0 2.0 collective-permute-start.4
  336.8 1.3 collective-permute-start.5
  338.1 3.3 collective-permute-done.5
  341.4 27.0 %all_to_all.50 = f32[64,1,3,131]{3,1,2,0:T(1,128)S(1)} all-to-all(f32[64,1,3,131]{3,1,2,0:T(1,128)S(1)} %broadcast_in_dim.112), channel_id=1, replica_groups=mesh['src'=64,'ccd'=8] {'src'}, dimensions={0} | all-to-all | bytes 201216 | tf_op jit(solution)/shard_map/all_to_all | solution.py:20
  368.7 5.0 %while.83 = (s32[]{:T(128)}, f32[4,16,12,128]{3,2,1,0:T(8,128)S(1)}, f32[4,16,12,128]{3,1,0,2:T(8,128)S(1)}, s32[4,16,128]{2,1,0:T(8,128)S(1)}, s32[]{:T(128)}) while((s32[]{:T(128)}, f32[4,16,12,128]{3,2,1,0:T(8,128)S(1)}, f32[4,16,12,128]{3,1,0,2:T(8,128)S(1)}, s32[4,16,128]{2,1,0:T(8,128)S(1)}, s32[]{:T(128)}) %tuple.279), condition=%wide.region_30.31_spmd.clone, body=%wide.region_29.30_spmd.clone.sunk | while | flops 38010880 | bytes 450633 | solution.py:153
  368.7 1.2 fusion.106
  370.0 1.2 fusion.106
  371.2 1.2 fusion.106
  372.4 1.2 fusion.106
  (206 shorter events, 34.0 us)
Async XLA Ops:
  0.6 7.2 %copy-start.5 = (s32[8192]{0:T(1024)S(1)}, s32[8192]{0:T(1024)}, u32[]{:S(2)}) copy-start(s32[8192]{0:T(1024)} %param.27) | copy-start | bytes 98308
  5.2 58.6 %copy-start.2 = (f32[5,8192]{1,0:T(8,128)S(1)}, f32[5,8192]{1,0:T(8,128)}, u32[]{:S(2)}) copy-start(f32[5,8192]{1,0:T(8,128)} %param.22) | copy-start | bytes 491524
  7.9 58.6 %copy-start.3 = (f32[8192]{0:T(1024)S(1)}, f32[8192]{0:T(1024)}, u32[]{:S(2)}) copy-start(f32[8192]{0:T(1024)} %param.25) | copy-start | bytes 98308
  53.5 22.5 %all-to-all-start = ((f32[8,20,1024]{2,1,0:T(8,128)}), f32[8,20,1024]{2,1,0:T(8,128)S(1)}, u32[]{:S(2)}, u32[]{:S(2)}) async-start(f32[8,20,1024]{2,1,0:T(8,128)} %broadcast_in_dim.66), calls=%async_computation | async-start | bytes 1572864 | tf_op jit(solution)/shard_map/all_to_all | solution.py:20
  76.4 33.2 %copy-start.6 = (f32[5,1024]{1,0:T(8,128)}, f32[5,1024]{1,0:T(8,128)S(1)}, u32[]{:S(2)}) copy-start(f32[5,1024]{1,0:T(8,128)S(1)} %stack.92) | copy-start | bytes 61444
  104.4 5.2 %copy-start.4 = (f32[8192]{0:T(1024)S(1)}, f32[8192]{0:T(1024)}, u32[]{:S(2)}) copy-start(f32[8192]{0:T(1024)} %param.23) | copy-start | bytes 98308
  104.4 5.2 %copy-start.8 = (s32[1,1,64]{2,1,0:T(1,128)S(1)}, s32[1,1,64]{2,1,0:T(1,128)}, u32[]{:S(2)}) copy-start(s32[1,1,64]{2,1,0:T(1,128)} %param.29) | copy-start | bytes 772
  104.4 5.3 %copy-start = (f32[3,8192]{1,0:T(4,128)S(1)}, f32[3,8192]{1,0:T(4,128)}, u32[]{:S(2)}) copy-start(f32[3,8192]{1,0:T(4,128)} %param.26) | copy-start | bytes 294916
  109.6 0.8 copy-start.1
  171.1 3.5 collective-permute-start
  174.6 4.6 %collective-permute-start.1 = (f32[3,3]{1,0:T(4,128)S(1)}, f32[3,3]{1,0:T(4,128)S(1)}, u32[]{:S(2)}, u32[]{:S(2)}) collective-permute-start(f32[3,3]{1,0:T(4,128)S(1)} %bitcast.270), channel_id=1, source_target_pairs={{8,0},{16,8},{24,16},{32,24},{40,32},{48,40},{56,48},{64,56},{72,6... | collective-permute-start | bytes 116 | tf_op jit(solution)/shard_map/ppermute | solution.py:31
  179.9 26.9 %all-to-all-start.3 = ((f32[64,1,3,131]{3,1,2,0:T(1,128)}), f32[64,1,3,131]{3,1,2,0:T(1,128)S(1)}, u32[]{:S(2)}, u32[]{:S(2)}) async-start(f32[64,1,3,131]{3,1,2,0:T(1,128)} %broadcast_in_dim.108), calls=%async_computation.3 | async-start | bytes 393216 | tf_op jit(solution)/shard_map/all_to_all | solution.py:20
  252.7 2.8 collective-permute-start.2
  255.5 4.6 %collective-permute-start.3 = (f32[3,3]{1,0:T(4,128)S(1)}, f32[3,3]{1,0:T(4,128)S(1)}, u32[]{:S(2)}, u32[]{:S(2)}) collective-permute-start(f32[3,3]{1,0:T(4,128)S(1)} %bitcast.269), channel_id=1, source_target_pairs={{8,0},{16,8},{24,16},{32,24},{40,32},{48,40},{56,48},{64,56},{72,6... | collective-permute-start | bytes 116 | tf_op jit(solution)/shard_map/ppermute | solution.py:31
  260.9 27.2 %all-to-all-start.6 = ((f32[64,1,3,131]{3,1,2,0:T(1,128)}), f32[64,1,3,131]{3,1,2,0:T(1,128)S(1)}, u32[]{:S(2)}, u32[]{:S(2)}) async-start(f32[64,1,3,131]{3,1,2,0:T(1,128)} %broadcast_in_dim.110), calls=%async_computation.6 | async-start | bytes 393216 | tf_op jit(solution)/shard_map/all_to_all | solution.py:20
  334.0 2.8 collective-permute-start.4
  336.7 38.1 %copy-start.7 = (f32[3,128]{1,0:T(4,128)}, f32[3,128]{1,0:T(4,128)S(1)}, u32[]{:S(2)}) copy-start(f32[3,128]{1,0:T(4,128)S(1)} %fusion.73) | copy-start | bytes 4612
  336.8 4.6 %collective-permute-start.5 = (f32[3,3]{1,0:T(4,128)S(1)}, f32[3,3]{1,0:T(4,128)S(1)}, u32[]{:S(2)}, u32[]{:S(2)}) collective-permute-start(f32[3,3]{1,0:T(4,128)S(1)} %bitcast.271), channel_id=1, source_target_pairs={{8,0},{16,8},{24,16},{32,24},{40,32},{48,40},{56,48},{64,56},{72,6... | collective-permute-start | bytes 116 | tf_op jit(solution)/shard_map/ppermute | solution.py:31
where the time goes:
time: 378 us; the launch traced here: 375 us
  blocking collectives  144 us (38%)
  other arithmetic  58.5 us (15%)
  waiting for transfers between devices  54 us (14%)
  local copies, waits for them, and re-layouts  43.9 us (12%)
  starting transfers between devices  42.6 us (11%)
  matrix products  29.1 us (8%)
    all_to_all x3, blocking collectives, sent_and_summed(): lax.all_to_all(tiles, axis, split_axis=0, concat_axis=0, tiled=True)  83 us
    all_to_all x4, blocking collectives, sent_to_all(): return lax.all_to_all(copies, axis, split_axis=0, concat_axis=0, tiled=True)  61.4 us
    scatter-add x1, other arithmetic, on_device(): jax.ops.segment_sum(row_moments(design, observed, weight_live).T, source_...  44.4 us
    all_to_all x3, waiting for transfers between devices, sent_to_all(): return lax.all_to_all(copies, axis, split_axis=0, concat_axis=0, tiled=True)  41.9 us
    all_to_all x3, starting transfers between devices, sent_to_all(): return lax.all_to_all(copies, axis, split_axis=0, concat_axis=0, tiled=True)  31.9 us
    gather x1, local copies, waits for them, and re-layouts, on_device(): fitted = jnp.sum(design * jnp.take(params, source_index, axis=1), 0)  27.7 us
    dot_general x16, matrix products, add_block(): jnp.einsum('gcr,grk->gck', values_blk, onehot, precision=lax.Precision.HI...  14.8 us
    dot_general x12, matrix products, pick_block(): jnp.einsum('gck,grk->gcr', windows_blk, onehot, precision=lax.Precision.H...  14.3 us
  transfers between devices with their start and end apart: 9, of which 9 were waited for; matrix products, arithmetic and copies ran while one was open for 1% of the time, Pallas kernels for 0%

commit v1 on v0

v1 whole, which is shorter than its diff:
```python
import functools

import jax
import jax.numpy as jnp
from jax import lax
from jax.experimental import pallas as pl
from jax.experimental.pallas import tpu as pltpu
from jax.sharding import PartitionSpec as P

F32 = jnp.float32
BF16 = jnp.bfloat16
MESH = pl.DeviceIdType.MESH
SRC_RIDGE = 1.0
ATT_RIDGE = 1.0
RELAX = 0.15
SWEEPS = 3
BLOCKS = 64
TILES = 65
HALF = 33
KNOTS = 8192
HALO = 6
PAIRS = [(0, 0), (0, 1), (0, 2), (1, 1), (1, 2), (2, 2)]
NT = (((1,), (1,)), ((), ()))
NN = (((1,), (0,)), ((), ()))


def moment_row(m, n):
    m, n = min(m, n), max(m, n)
    return {0: n, 4: n + 2, 1: 7 + n, 3: 10 + n, 2: 14 + n}[m]


def parts(value, count):
    out = []
    rest = value
    for _ in range(count - 1):
        top = rest.astype(BF16).astype(F32)
        out.append(top)
        rest = rest - top
    out.append(rest)
    return out


def solve_rows(row):
    factor = {}
    inverse = {}
    for j in range(5):
        for i in range(j, 5):
            running = row(moment_row(j, i)) + (SRC_RIDGE if i == j else 0.0)
            for k in range(j):
                running = running - factor[i, k] * factor[j, k]
            if i == j:
                inverse[j] = 1.0 / jnp.sqrt(running)
            else:
                factor[i, j] = running * inverse[j]
    forward = []
    for i in range(5):
        running = row(moment_row(i, 5))
        for k in range(i):
            running = running - factor[i, k] * forward[k]
        forward.append(running * inverse[i])
    solved = [None] * 5
    for i in reversed(range(5)):
        running = forward[i]
        for k in range(i + 1, 5):
            running = running - factor[k, i] * solved[k]
        solved[i] = running * inverse[i]
    return solved


def kernel(
    design, obs, wt, ph, ax, sidx, kidx, cnt,
    params_o, att_o, res_o,
    otlo, otk, bb, wl, ax8, lhs, acc, mom, momr, par,
    nloc, nhalf, nsum, nr, npc, nz, nf,
    rloc, rhalf, rsum, rr, rpc, rz, cp, cb, resid,
    ma_s, ma_r, pa_s, pa_r, nh_s, nh_r, np_s, np_r, nz_s, nz_r, ng_s, ng_r,
    rh_s, rh_r, rp_s, rp_r, rz_s, rz_r, cg_s, cg_r,
):
    src = lax.axis_index("src")
    ccd = lax.axis_index("ccd")
    z, y = src // 4, src % 4
    x, core = ccd // 2, ccd % 2
    chip = y * 4 + x
    pid = core * 16 + chip

    def plane(ky, kx, kc):
        return z * 4 + (y + ky) % 4, ((x + kx) % 4) * 2 + (core + kc) % 2

    def along(kz):
        return ((z + kz) % 16) * 4 + y, ccd

    steps16 = [(ky, kx) for ky in range(4) for kx in range(4) if (ky, kx) != (0, 0)]
    steps32 = [(ky, kx, kc) for ky in range(4) for kx in range(4) for kc in range(2) if (ky, kx, kc) != (0, 0, 0)]
    zsteps = [8, 7, 9, 6, 10, 5, 11, 4, 12, 3, 13, 2, 14, 1, 15]
    started = []

    def send(a, b, ssem, rsem, to):
        copy = pltpu.make_async_remote_copy(
            src_ref=a, dst_ref=b, send_sem=ssem, recv_sem=rsem, device_id=to, device_id_type=MESH
        )
        copy.start()
        started.append(copy)
        return copy

    barrier = pltpu.get_barrier_semaphore()
    for k in steps32:
        pl.semaphore_signal(barrier, inc=1, device_id=plane(*k), device_id_type=MESH)
    for k in zsteps:
        pl.semaphore_signal(barrier, inc=1, device_id=along(k), device_id_type=MESH)

    lane = lax.broadcasted_iota(jnp.int32, (8, 128), 1)
    lane1 = lax.broadcasted_iota(jnp.int32, (1, 128), 1)
    sub = lax.broadcasted_iota(jnp.int32, (8, 128), 0)
    iota256 = lax.broadcasted_iota(jnp.int32, (256, 128), 0)
    iota128 = lax.broadcasted_iota(jnp.int32, (128, 128), 0)

    def cols(d):
        return pl.ds(pl.multiple_of(d * 128, 128), 128)

    acc[...] = jnp.zeros_like(acc)

    def moments_step(t, carry):
        for b in range(8):
            d = t * 8 + b
            s_row = sidx[pl.ds(d, 1), :]
            low = s_row & 255
            high = jnp.broadcast_to(s_row >> 8, (72, 128))
            otlo[:, cols(d)] = jnp.where(iota256 == low, 1.0, 0.0).astype(BF16)
            w = jnp.where(lane1 < cnt[0, d], wt[pl.ds(d, 1), :], 0.0)
            wl[pl.ds(d, 1), :] = w
            e = design[:, cols(d)]
            o = obs[pl.ds(d, 1), :]
            ea = jnp.concatenate([e, o, e[4:5], o], 0)
            eb = jnp.concatenate([e[1:5], o, e[3:5], o], 0)
            ec = jnp.concatenate([e[2:5], o, e[2:5], o], 0)
            g = jnp.concatenate(
                [
                    ea * jnp.where(sub < 6, e[0:1] * w, e[4:5] * w),
                    eb * jnp.where(sub < 5, e[1:2] * w, e[3:4] * w),
                    ec * (e[2:3] * w),
                ],
                0,
            )
            stacked = jnp.concatenate(parts(g, 3), 0)
            masked = [jnp.where(high == h, stacked, 0.0) for h in range(4)]
            lhs[:, b * 128 : (b + 1) * 128] = jnp.concatenate(masked, 0).astype(BF16)
        window = otlo[:, pl.ds(pl.multiple_of(t * 1024, 1024), 1024)]
        acc[...] += lax.dot_general(lhs[...], window, NT, preferred_element_type=F32)
        return carry

    lax.fori_loop(0, 8, moments_step, 0)
    for h in range(4):
        total = acc[72 * h : 72 * h + 24] + acc[72 * h + 24 : 72 * h + 48] + acc[72 * h + 48 : 72 * h + 72]
        mom[2 * h] = total[:, :128]
        mom[2 * h + 1] = total[:, 128:]

    pl.semaphore_wait(barrier, len(steps32) + len(zsteps))
    mom_copies = []
    for k in range(1, 8):
        to = (ccd + k) % 8
        mom_copies.append(send(mom.at[to], momr.at[k - 1], ma_s.at[k - 1], ma_r.at[k - 1], (src, to)))

    u = ph[...]
    rem = 1.0 - u
    sq = u * u
    cu = sq * u
    basis = [
        rem * rem * rem / 6.0,
        (3.0 * cu - 6.0 * sq + 4.0) / 6.0,
        (-3.0 * cu + 3.0 * sq + 3.0 * u + 1.0) / 6.0,
        cu / 6.0,
    ]
    bbid = {}
    for i in range(4):
        bb[i] = basis[i]
    for i in range(4):
        for j in range(i, 4):
            bbid[i, j] = 4 + len(bbid)
            bb[bbid[i, j]] = basis[i] * basis[j]
    ax8[0:3, :] = ax[...]
    ax8[3:4, :] = jnp.zeros((1, KNOTS), F32)
    ax8[4:7, :] = ax[...]
    ax8[7:8, :] = jnp.zeros((1, KNOTS), F32)

    lane24 = lax.broadcasted_iota(jnp.int32, (24, 128), 1)

    def spread_shift(value, shift):
        lanes = lax.broadcasted_iota(jnp.int32, value.shape, 1)
        turned = pltpu.roll(value, shift, 1)
        return jnp.where(lanes >= shift, turned, 0.0), jnp.where(lanes < shift, turned, 0.0)

    def normal_step(t, carry):
        for b in range(8):
            d = t * 8 + b
            hot = jnp.where(iota128 == kidx[pl.ds(d, 1), :], 1.0, 0.0).astype(BF16)
            otk[d] = hot
            w = wl[pl.ds(d, 1), :]
            a = [jnp.broadcast_to(ax[i : i + 1, cols(d)], (8, 128)) for i in range(3)]
            wa = [w * a[i] for i in range(3)]
            left = jnp.where(sub < 3, wa[0], jnp.where(sub < 5, wa[1], wa[2]))
            right = jnp.where(
                sub == 0, a[0], jnp.where((sub == 1) | (sub == 3), a[1], a[2])
            )
            base = left * right
            tails = [
                jnp.where(sub == 6, wa[0] * a[0], wa[0] * a[1]),
                jnp.where(sub == 6, wa[0] * a[2], wa[1] * a[1]),
                jnp.where(sub == 6, wa[1] * a[2], wa[2] * a[2]),
            ]

            def term(i, j):
                return bb[bbid[i, j], pl.ds(d, 1), :]

            only = jnp.where(sub < 6, base, 0.0)
            groups = [jnp.where(sub < 6, base * term(0, o), tails[o] * term(0, 3)) for o in range(3)]
            groups += [only * term(1, 1), only * term(1, 2), only * term(1, 3)]
            groups += [only * term(2, 2), only * term(2, 3), only * term(3, 3)]
            stacked = jnp.concatenate(groups, 0)
            both = jnp.concatenate(parts(stacked, 2), 0).astype(BF16)
            sums = lax.dot_general(both, hot, NT, preferred_element_type=F32)
            sums = sums[:72] + sums[72:]
            c0, v0 = spread_shift(sums[0:24], HALO)
            c1, v1 = spread_shift(sums[24:48], HALO + 1)
            c2, v2 = spread_shift(sums[48:64], HALO + 2)
            c3, v3 = spread_shift(sums[64:72], HALO + 3)
            zeros8 = jnp.zeros((8, 128), F32)
            zeros16 = jnp.zeros((16, 128), F32)
            here = c0 + c1 + jnp.concatenate([c2, zeros8], 0) + jnp.concatenate([c3, zeros16], 0)
            nloc[d] = here + carry
            carry = v0 + v1 + jnp.concatenate([v2, zeros8], 0) + jnp.concatenate([v3, zeros16], 0)
        return carry

    nloc[BLOCKS] = lax.fori_loop(0, 8, normal_step, jnp.zeros((24, 128), F32))
    mate = (src, x * 2 + (core + 1) % 2)
    nhalf_copy = send(nloc.at[pl.ds(32 * ((core + 1) % 2), HALF)], nhalf, nh_s, nh_r, mate)

    for copy in mom_copies:
        copy.wait_recv()
    whole = mom[ccd]
    for k in range(7):
        whole = whole + momr[k]
    solved = solve_rows(lambda r: whole[r : r + 1])
    par[ccd] = jnp.concatenate(solved + [jnp.zeros((3, 128), F32)], 0)
    for k in range(1, 8):
        send(par.at[ccd], par.at[ccd], pa_s.at[k - 1], pa_r.at[k - 1], (src, (ccd + k) % 8))

    nhalf_copy.wait_recv()
    for i in range(HALF):
        nsum[i] = nloc[32 * core + i] + nhalf[i]
    n_copies = []
    for i, (ky, kx) in enumerate(steps16):
        there = ((y + ky) % 4) * 4 + (x + kx) % 4
        n_copies.append(send(nsum.at[pl.ds(2 * there, 3)], nr.at[i], np_s.at[i], np_r.at[i], plane(ky, kx, 0)))

    for k in range(1, 8):
        sender = (ccd + 8 - k) % 8
        pltpu.make_async_remote_copy(
            src_ref=par.at[sender], dst_ref=par.at[sender], send_sem=pa_s.at[k - 1], recv_sem=pa_r.at[k - 1],
            device_id=(src, sender), device_id_type=MESH,
        ).wait_recv()
    for c in range(8):
        params_o[:, c * 128 : (c + 1) * 128] = par[c, 0:5]
    table = jnp.concatenate([jnp.concatenate([par[2 * h], par[2 * h + 1]], 1) for h in range(4)], 0)
    table = jnp.concatenate(parts(table, 3), 0).astype(BF16)

    def residual_step(t, carry):
        window = otlo[:, pl.ds(pl.multiple_of(t * 1024, 1024), 1024)]
        picked = lax.dot_general(table, window, NN, preferred_element_type=F32)
        picked = picked[0:32] + picked[32:64] + picked[64:96]
        for b in range(8):
            d = t * 8 + b
            high = jnp.broadcast_to(sidx[pl.ds(d, 1), :] >> 8, (8, 128))
            own = picked[:, b * 128 : (b + 1) * 128]
            chosen = own[0:8]
            for h in range(1, 4):
                chosen = jnp.where(high == h, own[8 * h : 8 * h + 8], chosen)
            fitted = jnp.sum(chosen[0:5] * design[:, cols(d)], 0, keepdims=True)
            r = jnp.where(lane1 < cnt[0, d], obs[pl.ds(d, 1), :] - fitted, 0.0)
            resid[pl.ds(d, 1), :] = r
            wr = wl[pl.ds(d, 1), :] * r
            a = ax8[:, cols(d)]
            upper = sub < 4
            pair01 = a * jnp.where(upper, wr * bb[0, pl.ds(d, 1), :], wr * bb[1, pl.ds(d, 1), :])
            pair23 = a * jnp.where(upper, wr * bb[2, pl.ds(d, 1), :], wr * bb[3, pl.ds(d, 1), :])
            stacked = jnp.concatenate([pair01, pair23], 0)
            split = jnp.concatenate(parts(stacked, 3), 0).astype(BF16)
            sums = lax.dot_general(split, otk[d], NT, preferred_element_type=F32)
            sums = sums[0:16] + sums[16:32] + sums[32:48]
            here = carry
            over = jnp.zeros((8, 128), F32)
            for g in range(2):
                value = sums[8 * g : 8 * g + 8]
                first, second = HALO + 2 * g, HALO + 2 * g + 1
                turned = jnp.where(upper, pltpu.roll(value, first, 1), pltpu.roll(value, second, 1))
                limit = jnp.where(upper, first, second)
                here = here + jnp.where(lane >= limit, turned, 0.0)
                over = over + jnp.where(lane < limit, turned, 0.0)
            folded = here + pltpu.roll(here, 4, 0)
            rloc[d] = folded[0:4]
            carry = over
        return carry

    last = lax.fori_loop(0, 8, residual_step, jnp.zeros((8, 128), F32))
    last = last + pltpu.roll(last, 4, 0)
    rloc[BLOCKS] = last[0:4]

    rhalf_copy = send(rloc.at[pl.ds(32 * ((core + 1) % 2), HALF)], rhalf, rh_s, rh_r, mate)
    rhalf_copy.wait_recv()
    for i in range(HALF):
        rsum[i] = rloc[32 * core + i] + rhalf[i]
    r_copies = []
    for i, (ky, kx) in enumerate(steps16):
        there = ((y + ky) % 4) * 4 + (x + kx) % 4
        r_copies.append(send(rsum.at[pl.ds(2 * there, 3)], rr.at[i], rp_s.at[i], rp_r.at[i], plane(ky, kx, 0)))

    for copy in n_copies:
        copy.wait_recv()
    for t in range(3):
        total = nsum[2 * chip + t]
        for i in range(15):
            total = total + nr[i, t]
        for g in range(3):
            npc[3 * t + g] = total[8 * g : 8 * g + 8]
    owners = [(16 * g) // 9 for g in range(9)]
    mine = (9 * z + 15) // 16
    is_owner = (16 * mine) // 9 == z
    for g, owner in enumerate(owners):
        step = (owner + 16 - z) % 16

        @pl.when(owner != z)
        def _(g=g, owner=owner, step=step):
            pltpu.make_async_remote_copy(
                src_ref=npc.at[g], dst_ref=nz.at[step - 1], send_sem=nz_s.at[g], recv_sem=nz_r.at[step - 1],
                device_id=(owner * 4 + y, ccd), device_id_type=MESH,
            ).start()

    for copy in r_copies:
        copy.wait_recv()
    for t in range(3):
        total = rsum[2 * chip + t]
        for i in range(15):
            total = total + rr[i, t]
        rpc[t] = total
    rz_copies = []
    for kz in zsteps:
        rz_copies.append(send(rpc, rz.at[kz - 1], rz_s.at[kz - 1], rz_r.at[kz - 1], along(kz)))

    @pl.when(is_owner)
    def _():
        total = npc[mine]
        for k in range(15):
            pltpu.make_async_remote_copy(
                src_ref=npc.at[0], dst_ref=nz.at[k], send_sem=nz_s.at[0], recv_sem=nz_r.at[k],
                device_id=along(k + 1), device_id_type=MESH,
            ).wait_recv()
            total = total + nz[k]
        nf[mine] = total
        for k in zsteps:
            pltpu.make_async_remote_copy(
                src_ref=nf.at[mine], dst_ref=nf.at[mine], send_sem=ng_s.at[k - 1], recv_sem=ng_r.at[mine],
                device_id=along(k), device_id_type=MESH,
            ).start()

    for copy in rz_copies:
        copy.wait_recv()
    rows = []
    for t in range(3):
        total = rpc[t]
        for i in range(15):
            total = total + rz[i, t]
        rows.append(total)
    rhs4 = jnp.concatenate(rows, 1)
    for g, owner in enumerate(owners):

        @pl.when(owner != z)
        def _(g=g, owner=owner):
            pltpu.make_async_remote_copy(
                src_ref=nf.at[g], dst_ref=nf.at[g], send_sem=ng_s.at[0], recv_sem=ng_r.at[g],
                device_id=(owner * 4 + y, ccd), device_id_type=MESH,
            ).wait_recv()

    def wide(row):
        return jnp.broadcast_to(row, (8, 384))

    def band(o, pair):
        g, s = (o, pair) if o < 3 else (pair // 2, 6 + pair % 2)
        return wide(jnp.concatenate([nf[3 * t + g, s : s + 1] for t in range(3)], 1))

    bands = [{} for _ in range(4)]
    for o in range(4):
        for p, (a, b) in enumerate(PAIRS):
            bands[o][a, b] = bands[o][b, a] = band(o, p)
    inside = lax.broadcasted_iota(jnp.int32, (8, 384), 1) < KNOTS + HALO - 256 * pid
    rhs = [wide(rhs4[i : i + 1]) for i in range(3)]
    scale = [RELAX / (ATT_RIDGE + bands[0][i, i]) for i in range(3)]
    coef = [jnp.where(inside, rhs[i] * scale[i], 0.0) for i in range(3)]
    for _ in range(1, SWEEPS):
        ahead = [[pltpu.roll(coef[i], 384 - o, 1) for i in range(3)] for o in range(1, 4)]
        fresh = []
        for i in range(3):
            product = coef[i] * ATT_RIDGE
            for k in range(3):
                product = product + bands[0][i, k] * coef[k]
            for o in range(1, 4):
                back = bands[o][i, 0] * coef[0] + bands[o][i, 1] * coef[1] + bands[o][i, 2] * coef[2]
                product = product + pltpu.roll(back, o, 1)
                for k in range(3):
                    product = product + bands[o][i, k] * ahead[o - 1][k]
            fresh.append(jnp.where(inside, coef[i] + scale[i] * (rhs[i] - product), 0.0))
        coef = fresh
    cp[:, 3:4, :] = jnp.zeros((2, 1, 128), F32)
    for i in range(3):
        moved = pltpu.roll(coef[i], 384 - HALO, 1)
        for t in range(2):
            cp[t, i : i + 1] = moved[0:1, t * 128 : (t + 1) * 128]
    for t in range(2):
        cb[2 * pid + t] = cp[t]
    cb[BLOCKS] = jnp.zeros((4, 128), F32)
    for i, k in enumerate(steps32):
        send(cp, cb.at[pl.ds(2 * pid, 2)], cg_s.at[i], cg_r.at[i], plane(*k))
    for i, (ky, kx, kc) in enumerate(steps32):
        sy, sx, sc = (y + 4 - ky) % 4, (x + 4 - kx) % 4, (core + 2 - kc) % 2
        slot = cb.at[pl.ds(2 * (sc * 16 + sy * 4 + sx), 2)]
        pltpu.make_async_remote_copy(
            src_ref=cp, dst_ref=slot, send_sem=cg_s.at[i], recv_sem=cg_r.at[i],
            device_id=(z * 4 + sy, sx * 2 + sc), device_id_type=MESH,
        ).wait_recv()
    att_o[...] = cb[src][0:3]

    def final_step(t, carry):
        for b in range(8):
            d = t * 8 + b
            now = jnp.concatenate([cb[d], cb[d + 1]], 0)
            shifted = []
            for j in range(4):
                turned = now if j == 0 else pltpu.roll(now, 128 - j, 1)
                up = pltpu.roll(turned, 4, 0)
                shifted.append(jnp.where(lane < 128 - j, turned, up))
            pair01 = jnp.where(sub < 4, shifted[0], pltpu.roll(shifted[1], 4, 0))
            pair23 = jnp.where(sub < 4, shifted[2], pltpu.roll(shifted[3], 4, 0))
            stacked = jnp.concatenate([pair01, pair23], 0)
            split = jnp.concatenate(parts(stacked, 3), 0).astype(BF16)
            picked = lax.dot_general(split, otk[d], NN, preferred_element_type=F32)
            picked = picked[0:16] + picked[16:32] + picked[32:48]
            upper = sub < 4
            b01 = jnp.where(upper, bb[0, pl.ds(d, 1), :], bb[1, pl.ds(d, 1), :])
            b23 = jnp.where(upper, bb[2, pl.ds(d, 1), :], bb[3, pl.ds(d, 1), :])
            terms = ax8[:, cols(d)] * (picked[0:8] * b01 + picked[8:16] * b23)
            predicted = jnp.sum(terms, 0, keepdims=True)
            res_o[pl.ds(d, 1), :] = jnp.where(
                lane1 < cnt[0, d], resid[pl.ds(d, 1), :] - predicted, 0.0
            )
        return carry

    lax.fori_loop(0, 8, final_step, 0)

    for copy in started:
        copy.wait_send()
    for g, owner in enumerate(owners):

        @pl.when(owner != z)
        def _(g=g, owner=owner):
            pltpu.make_async_remote_copy(
                src_ref=npc.at[g], dst_ref=nz.at[0], send_sem=nz_s.at[g], recv_sem=nz_r.at[0],
                device_id=(owner * 4 + y, ccd), device_id_type=MESH,
            ).wait_send()

    @pl.when(is_owner)
    def _():
        for k in zsteps:
            pltpu.make_async_remote_copy(
                src_ref=nf.at[mine], dst_ref=nf.at[mine], send_sem=ng_s.at[k - 1], recv_sem=ng_r.at[mine],
                device_id=along(k), device_id_type=MESH,
            ).wait_send()


def on_device(design, observed, weight, phase_frac, axis_factors, source_index, knot_index, counts):
    dma = pltpu.SemaphoreType.DMA
    vm = lambda *shape: pltpu.VMEM(shape, F32)
    vmem = pl.BlockSpec(memory_space=pltpu.VMEM)
    square = lambda v: v.reshape(64, 128)
    params, attitude, residual = pl.pallas_call(
        kernel,
        out_shape=(
            jax.ShapeDtypeStruct((5, 1024), F32),
            jax.ShapeDtypeStruct((3, 128), F32),
            jax.ShapeDtypeStruct((64, 128), F32),
        ),
        in_specs=[vmem] * 7 + [pl.BlockSpec(memory_space=pltpu.SMEM)],
        out_specs=(vmem, vmem, vmem),
        scratch_shapes=[
            pltpu.VMEM((256, 8192), BF16),
            pltpu.VMEM((64, 128, 128), BF16),
            vm(14, 64, 128), vm(64, 128), vm(8, 8192),
            pltpu.VMEM((288, 1024), BF16),
            vm(288, 256), vm(8, 24, 128), vm(7, 24, 128), vm(8, 8, 128),
            vm(TILES, 24, 128), vm(HALF, 24, 128), vm(HALF, 24, 128), vm(15, 3, 24, 128),
            vm(9, 8, 128), vm(15, 8, 128), vm(9, 8, 128),
            vm(TILES, 4, 128), vm(HALF, 4, 128), vm(HALF, 4, 128), vm(15, 3, 4, 128),
            vm(3, 4, 128), vm(15, 3, 4, 128), vm(2, 4, 128), vm(TILES, 4, 128), vm(64, 128),
            dma((7,)), dma((7,)), dma((7,)), dma((7,)),
            dma, dma, dma((15,)), dma((15,)), dma((9,)), dma((15,)), dma((15,)), dma((9,)),
            dma, dma, dma((15,)), dma((15,)), dma((15,)), dma((15,)), dma((31,)), dma((31,)),
        ],
        compiler_params=pltpu.CompilerParams(
            collective_id=0, has_side_effects=True, vmem_limit_bytes=48 * 1024 * 1024
        ),
    )(
        design, square(observed), square(weight), square(phase_frac), axis_factors,
        square(source_index), square(knot_index), counts.reshape(1, 64),
    )
    return params, attitude, residual.reshape(8192)


def solution(mesh):
    rows = P(("src", "ccd"))
    wide = P(None, ("src", "ccd"))
    in_specs = (wide, rows, rows, rows, wide, rows, rows, P("src", "ccd", None))
    out_specs = (P(None, "src"), P(None, "src"), rows)
    return jax.shard_map(on_device, mesh=mesh, in_specs=in_specs, out_specs=out_specs, check_vma=False)
```

time: 378 us -> 67.6 us (0.18)
  blocking collectives: 144 us -> 0 us
  other arithmetic: 58.5 us -> 0 us
  Pallas kernels: 0 us -> 58.3 us
  waiting for transfers between devices: 54 us -> 0 us
  starting transfers between devices: 42.6 us -> 0 us
  local copies, waits for them, and re-layouts: 43.9 us -> 8.1 us
  matrix products: 29.1 us -> 0 us
    all_to_all x7 -> x0, blocking collectives: 144 us -> none  [the longest x3 83 us: sent_and_summed(): lax.all_to_all(tiles, axis, split_axis=0, concat_axis=0, tiled=True)]
    pallas_call x0 -> x1, Pallas kernels: none -> 58.3 us  [on_device(): pl.pallas_call(kernel, out_shape=(jax.ShapeDtypeStruct((5, 1024), F32), j...]
    scatter-add x1 -> x0, other arithmetic: 44.4 us -> none  [on_device(): jax.ops.segment_sum(row_moments(design, observed, weight_live).T, source_...]
    all_to_all x3 -> x0, waiting for transfers between devices: 41.9 us -> none  [sent_to_all(): return lax.all_to_all(copies, axis, split_axis=0, concat_axis=0, tiled=True)]
    all_to_all x3 -> x0, starting transfers between devices: 31.9 us -> none  [sent_to_all(): return lax.all_to_all(copies, axis, split_axis=0, concat_axis=0, tiled=True)]
    dot_general x28 -> x0, matrix products: 29.1 us -> none  [the longest x16 14.8 us: add_block(): jnp.einsum('gcr,grk->gck', values_blk, onehot, precision=lax.Precision.HI...]
    gather x1 -> x0, local copies, waits for them, and re-layouts: 27.7 us -> none  [on_device(): fitted = jnp.sum(design * jnp.take(params, source_index, axis=1), 0)]
    ppermute x6 -> x0, waiting for transfers between devices: 12 us -> none  [passed_along(): return lax.ppermute(block, axis, route)]
  transfers between devices with their start and end apart: 9 -> 0, of which waited for: 9 -> 0; matrix products, arithmetic and copies ran while one was open for 1% -> 0% of each run, Pallas kernels for 0% -> 0%
where the time goes in v1:
time: 67.6 us; the launch traced here: 67.1 us
  Pallas kernels  58.3 us (86%)
  local copies, waits for them, and re-layouts  8.1 us (12%)
    pallas_call x1, Pallas kernels, on_device(): pl.pallas_call(kernel, out_shape=(jax.ShapeDtypeStruct((5, 1024), F32), j...  58.3 us
    unnamed x19, local copies, waits for them, and re-layouts  8.1 us

profile of v1, /device:TPU:1, one launch (start us, length us, event | category | flops | bytes accessed | tf_op | source)
XLA Modules:
  0.0 67.1 jit_solution(884139219537617630)
XLA Ops:
  0.6 0.0 copy-start.7
  0.6 0.6 copy-done.7
  1.3 0.0 copy-start
  1.3 0.9 %copy-done = f32[5,8192]{1,0:T(8,128)S(1)} copy-done((f32[5,8192]{1,0:T(8,128)S(1)}, f32[5,8192]{1,0:T(8,128)}, u32[]{:S(2)}) %copy-start) | copy-done | bytes 163864
  2.2 0.0 copy-start.1
  2.2 0.9 %copy-done.1 = f32[3,8192]{1,0:T(4,128)S(1)} copy-done((f32[3,8192]{1,0:T(4,128)S(1)}, f32[3,8192]{1,0:T(4,128)}, u32[]{:S(2)}) %copy-start.1) | copy-done | bytes 98328
  3.1 0.0 copy-start.2
  3.1 0.8 %copy-done.2 = f32[8192]{0:T(1024)S(1)} copy-done((f32[8192]{0:T(1024)S(1)}, f32[8192]{0:T(1024)}, u32[]{:S(2)}) %copy-start.2) | copy-done | bytes 32792
  3.9 0.0 copy-start.3
  3.9 0.8 %copy-done.3 = f32[8192]{0:T(1024)S(1)} copy-done((f32[8192]{0:T(1024)S(1)}, f32[8192]{0:T(1024)}, u32[]{:S(2)}) %copy-start.3) | copy-done | bytes 32792
  4.7 0.0 copy-start.4
  4.7 0.8 %copy-done.4 = f32[8192]{0:T(1024)S(1)} copy-done((f32[8192]{0:T(1024)S(1)}, f32[8192]{0:T(1024)}, u32[]{:S(2)}) %copy-start.4) | copy-done | bytes 32792
  5.4 0.0 copy-start.5
  5.4 0.8 %copy-done.5 = s32[8192]{0:T(1024)S(1)} copy-done((s32[8192]{0:T(1024)S(1)}, s32[8192]{0:T(1024)}, u32[]{:S(2)}) %copy-start.5) | copy-done | bytes 32792
  6.2 0.0 copy-start.6
  6.2 0.8 %copy-done.6 = s32[8192]{0:T(1024)S(1)} copy-done((s32[8192]{0:T(1024)S(1)}, s32[8192]{0:T(1024)}, u32[]{:S(2)}) %copy-start.6) | copy-done | bytes 32792
  6.9 58.3 %shard_map.103 = (f32[5,1024]{1,0:T(8,128)S(1)}, f32[3,128]{1,0:T(4,128)S(1)}, f32[64,128]{1,0:T(8,128)S(1)}) custom-call(f32[5,8192]{1,0:T(8,128)S(1)} %copy-done, f32[64,128]{1,0:T(8,128)S(1)} %bitcast.7, f32[64,128]{1,0:T(8,128)S(1)} %bitcast.8, f32[64,128]{1,0:T(8,128)S(1)} %bitcast.9, f32[3,8192]{1,0:T(4,128)S(1)} %copy-done.1, s32[64,128]{1,0:T(8,128)S(1)} %bitcast.10, ...), custom_call_target="tpu_custom_call" | custom-call | tf_op jit(solution)/shard_map/pallas_call | solution.py:482
  65.3 0.6 copy.14
  65.9 0.6 copy.15
  66.5 0.6 copy.16
Async XLA Ops:
  0.6 0.7 copy-start.7
  1.3 0.9 %copy-start = (f32[5,8192]{1,0:T(8,128)S(1)}, f32[5,8192]{1,0:T(8,128)}, u32[]{:S(2)}) copy-start(f32[5,8192]{1,0:T(8,128)} %design.1) | copy-start | bytes 491524
  2.2 0.9 %copy-start.1 = (f32[3,8192]{1,0:T(4,128)S(1)}, f32[3,8192]{1,0:T(4,128)}, u32[]{:S(2)}) copy-start(f32[3,8192]{1,0:T(4,128)} %ax.1) | copy-start | bytes 294916
  3.1 0.8 %copy-start.2 = (f32[8192]{0:T(1024)S(1)}, f32[8192]{0:T(1024)}, u32[]{:S(2)}) copy-start(f32[8192]{0:T(1024)} %param.9) | copy-start | bytes 98308
  3.9 0.8 %copy-start.3 = (f32[8192]{0:T(1024)S(1)}, f32[8192]{0:T(1024)}, u32[]{:S(2)}) copy-start(f32[8192]{0:T(1024)} %param.10) | copy-start | bytes 98308
  4.7 0.8 %copy-start.4 = (f32[8192]{0:T(1024)S(1)}, f32[8192]{0:T(1024)}, u32[]{:S(2)}) copy-start(f32[8192]{0:T(1024)} %param.11) | copy-start | bytes 98308
  5.4 0.8 %copy-start.5 = (s32[8192]{0:T(1024)S(1)}, s32[8192]{0:T(1024)}, u32[]{:S(2)}) copy-start(s32[8192]{0:T(1024)} %param.13) | copy-start | bytes 98308
  6.2 0.8 %copy-start.6 = (s32[8192]{0:T(1024)S(1)}, s32[8192]{0:T(1024)}, u32[]{:S(2)}) copy-start(s32[8192]{0:T(1024)} %param.14) | copy-start | bytes 98308

commit v2 on v1

v2 whole, which is shorter than its diff:
```python
import functools

import jax
import jax.numpy as jnp
from jax import lax
from jax.experimental import pallas as pl
from jax.experimental.pallas import tpu as pltpu
from jax.sharding import PartitionSpec as P

F32 = jnp.float32
BF16 = jnp.bfloat16
MESH = pl.DeviceIdType.MESH
SRC_RIDGE = 1.0
ATT_RIDGE = 1.0
RELAX = 0.15
SWEEPS = 3
BLOCKS = 64
TILES = 65
HALF = 33
KNOTS = 8192
HALO = 6
UNROLL = 16
PAIRS = [(0, 0), (0, 1), (0, 2), (1, 1), (1, 2), (2, 2)]
NT = (((1,), (1,)), ((), ()))
NN = (((1,), (0,)), ((), ()))


def moment_row(m, n):
    m, n = min(m, n), max(m, n)
    return {0: n, 4: n + 2, 1: 7 + n, 3: 10 + n, 2: 14 + n}[m]


def parts(value, count):
    out = []
    rest = value
    for _ in range(count - 1):
        top = rest.astype(BF16).astype(F32)
        out.append(top)
        rest = rest - top
    out.append(rest)
    return out


def solve_rows(row):
    factor = {}
    inverse = {}
    for j in range(5):
        for i in range(j, 5):
            running = row(moment_row(j, i)) + (SRC_RIDGE if i == j else 0.0)
            for k in range(j):
                running = running - factor[i, k] * factor[j, k]
            if i == j:
                inverse[j] = 1.0 / jnp.sqrt(running)
            else:
                factor[i, j] = running * inverse[j]
    forward = []
    for i in range(5):
        running = row(moment_row(i, 5))
        for k in range(i):
            running = running - factor[i, k] * forward[k]
        forward.append(running * inverse[i])
    solved = [None] * 5
    for i in reversed(range(5)):
        running = forward[i]
        for k in range(i + 1, 5):
            running = running - factor[k, i] * solved[k]
        solved[i] = running * inverse[i]
    return solved


def kernel(
    design_h, obs_h, wt_h, ph_h, ax_h, sidx_h, kidx_h, cnt_h,
    params_h, att_h, res_h,
    params_o, att_o, res_o, out_sem,
    design, obs, wt, ph, ax, sidx, kidx, cnt, in_sem,
    otlo, otk, bb, wl, ax8, lhs, acc, mom, momr, par,
    nloc, nhalf, nsum, nr, npc, nz, nf,
    rloc, rhalf, rsum, rr, rpc, rz, cp, cb, resid,
    ma_s, ma_r, pa_s, pa_r, nh_s, nh_r, np_s, np_r, nz_s, nz_r, ng_s, ng_r,
    rh_s, rh_r, rp_s, rp_r, rz_s, rz_r, cg_s, cg_r,
):
    src = lax.axis_index("src")
    ccd = lax.axis_index("ccd")
    z, y = src // 4, src % 4
    x, core = ccd // 2, ccd % 2
    chip = y * 4 + x
    pid = core * 16 + chip

    def plane(ky, kx, kc):
        return z * 4 + (y + ky) % 4, ((x + kx) % 4) * 2 + (core + kc) % 2

    def along(kz):
        return ((z + kz) % 16) * 4 + y, ccd

    steps16 = [(2, 2), (2, 1), (2, 3), (1, 2), (3, 2), (2, 0), (0, 2), (1, 1), (3, 3), (1, 3), (3, 1), (1, 0), (3, 0), (0, 1), (0, 3)]
    steps32 = [(ky, kx, kc) for ky, kx in steps16 for kc in (1, 0)] + [(0, 0, 1)]
    zsteps = [8, 7, 9, 6, 10, 5, 11, 4, 12, 3, 13, 2, 14, 1, 15]
    started = []

    loads = []
    held = (sidx, wt, design, obs, ph, ax, kidx)
    for i, (a, b) in enumerate(zip((sidx_h, wt_h, design_h, obs_h, ph_h, ax_h, kidx_h), held)):
        loads.append(pltpu.make_async_copy(a, b, in_sem.at[i]))
        loads[-1].start()

    loads.insert(0, pltpu.make_async_copy(cnt_h, cnt, in_sem.at[7]))
    loads[0].start()

    def send(a, b, ssem, rsem, to):
        copy = pltpu.make_async_remote_copy(
            src_ref=a, dst_ref=b, send_sem=ssem, recv_sem=rsem, device_id=to, device_id_type=MESH
        )
        copy.start()
        started.append(copy)
        return copy

    barrier = pltpu.get_barrier_semaphore()
    for k in steps32:
        pl.semaphore_signal(barrier, inc=1, device_id=plane(*k), device_id_type=MESH)
    for k in zsteps:
        pl.semaphore_signal(barrier, inc=1, device_id=along(k), device_id_type=MESH)

    lane = lax.broadcasted_iota(jnp.int32, (8, 128), 1)
    lane1 = lax.broadcasted_iota(jnp.int32, (1, 128), 1)
    sub = lax.broadcasted_iota(jnp.int32, (8, 128), 0)
    iota256 = lax.broadcasted_iota(jnp.int32, (256, 128), 0).astype(F32).astype(BF16)
    one, zero = jnp.ones((256, 128), BF16), jnp.zeros((256, 128), BF16)
    nought = jnp.zeros((64, 128), BF16)

    def cols(d):
        return pl.ds(pl.multiple_of(d * 128, 128), 128)

    def tall(row, count):
        packed = jnp.broadcast_to(row.astype(F32), (16, 128)).astype(BF16)
        return jnp.concatenate([packed] * count, 0)

    def hot(row):
        return jnp.where(iota256 == tall(row, 16), one, zero)

    for copy in loads[:5]:
        copy.wait()
    acc[...] = jnp.zeros_like(acc)

    def moments_step(t, carry):
        total = None
        for part in range(UNROLL // 8):
            for b in range(8):
                d = t * UNROLL + part * 8 + b
                s_row = sidx[pl.ds(d, 1), :]
                otlo[:, cols(d)] = hot(s_row & 255)
                high = tall(s_row >> 8, 4)
                w = jnp.where(lane1 < cnt[0, d], wt[pl.ds(d, 1), :], 0.0)
                wl[pl.ds(d, 1), :] = w
                e = jnp.concatenate([design[:, cols(d)], jnp.zeros((3, 128), F32)], 0)
                o = jnp.broadcast_to(obs[pl.ds(d, 1), :], (8, 128))
                e0, e1, e2, e3, e4 = [design[i : i + 1, cols(d)] for i in range(5)]
                down = pltpu.roll(e, 2, 0)
                ea = jnp.where(sub < 5, e, jnp.where(sub == 6, e4, o))
                eb = jnp.where(sub < 4, pltpu.roll(e, 7, 0), jnp.where((sub == 5) | (sub == 6), down, o))
                ec = jnp.where(sub < 3, pltpu.roll(e, 6, 0), jnp.where((sub > 3) & (sub < 7), down, o))
                ga = parts(w * ea * jnp.where(sub < 6, e0, e4), 3)
                gb = parts(w * eb * jnp.where(sub < 5, e1, e3), 3)
                gc = parts(w * ec * e2, 3)
                rows = [ga[0], gb[0], ga[1], gb[1], ga[2], gb[2], jnp.where(sub < 4, gc[0], gc[1]), gc[2]]
                stacked = jnp.concatenate(rows, 0).astype(BF16)
                for h in range(4):
                    masked = jnp.where(high == jnp.full((64, 128), h, BF16), stacked, nought)
                    lhs[part, 64 * h : 64 * h + 64, b * 128 : b * 128 + 128] = masked
            window = otlo[:, pl.ds(pl.multiple_of(t * UNROLL * 128 + part * 1024, 1024), 1024)]
            product = lax.dot_general(lhs[part], window, NT, preferred_element_type=F32)
            total = product if total is None else total + product
        acc[...] += total
        return carry

    lax.fori_loop(0, BLOCKS // UNROLL, moments_step, 0)
    for h in range(4):
        v = [acc[64 * h + 8 * i : 64 * h + 8 * i + 8] for i in range(8)]
        tail = v[6] + pltpu.roll(v[6], 4, 0) + v[7]
        total = jnp.concatenate([v[0] + v[2] + v[4], v[1] + v[3] + v[5], tail], 0)
        mom[2 * h] = total[:, :128]
        mom[2 * h + 1] = total[:, 128:]
    pl.semaphore_wait(barrier, len(steps32) + len(zsteps))
    mom_copies = []
    for k in (4, 5, 3, 2, 6, 7, 1):
        to = (ccd + k) % 8
        mom_copies.append(send(mom.at[to], momr.at[k - 1], ma_s.at[k - 1], ma_r.at[k - 1], (src, to)))

    for copy in loads[5:]:
        copy.wait()
    u = ph[...]
    rem = 1.0 - u
    sq = u * u
    cu = sq * u
    basis = [
        rem * rem * rem / 6.0,
        (3.0 * cu - 6.0 * sq + 4.0) / 6.0,
        (-3.0 * cu + 3.0 * sq + 3.0 * u + 1.0) / 6.0,
        cu / 6.0,
    ]
    bbid = {}
    for i in range(4):
        bb[i] = basis[i]
    for i in range(4):
        for j in range(i, 4):
            bbid[i, j] = 4 + len(bbid)
            bb[bbid[i, j]] = basis[i] * basis[j]
    ax8[0:3, :] = ax[...]
    ax8[3:4, :] = jnp.zeros((1, KNOTS), F32)
    ax8[4:7, :] = ax[...]
    ax8[7:8, :] = jnp.zeros((1, KNOTS), F32)

    def spread_shift(value, shift):
        lanes = lax.broadcasted_iota(jnp.int32, value.shape, 1)
        turned = pltpu.roll(value, shift, 1)
        return jnp.where(lanes >= shift, turned, 0.0), jnp.where(lanes < shift, turned, 0.0)

    def normal_step(t, carry):
        for pair in range(UNROLL // 2):
            p = t * (UNROLL // 2) + pair
            halves = []
            for b in range(2):
                d = 2 * p + b
                otk[p, :, b * 128 : b * 128 + 128] = hot(kidx[pl.ds(d, 1), :] + 128 * b)
                w = wl[pl.ds(d, 1), :]
                a = [jnp.broadcast_to(ax[i : i + 1, cols(d)], (8, 128)) for i in range(3)]
                wa = [w * a[i] for i in range(3)]
                left = jnp.where(sub < 3, wa[0], jnp.where(sub < 5, wa[1], wa[2]))
                right = jnp.where(sub == 0, a[0], jnp.where((sub == 1) | (sub == 3), a[1], a[2]))
                only = jnp.where(sub < 6, left * right, 0.0)
                tails = [
                    wa[0] * jnp.where(sub == 6, a[0], a[1]),
                    jnp.where(sub == 6, wa[0], wa[1]) * jnp.where(sub == 6, a[2], a[1]),
                    a[2] * jnp.where(sub == 6, wa[1], wa[2]),
                ]

                def term(i, j):
                    return bb[bbid[i, j], pl.ds(d, 1), :]

                last = term(0, 3)
                groups = [jnp.where(sub < 6, only * term(0, o), tails[o] * last) for o in range(3)]
                groups += [only * term(1, 1), only * term(1, 2), only * term(1, 3)]
                groups += [only * term(2, 2), only * term(2, 3), only * term(3, 3)]
                stacked = jnp.concatenate(groups, 0)
                halves.append(jnp.concatenate(parts(stacked, 2), 0).astype(BF16))
            both = jnp.concatenate(halves, 1)
            sums = lax.dot_general(both, otk[p], NT, preferred_element_type=F32)
            sums = sums[:72] + sums[72:]
            zeros8 = jnp.zeros((8, 128), F32)
            zeros16 = jnp.zeros((16, 128), F32)
            for b in range(2):
                own = sums[:, b * 128 : b * 128 + 128]
                c0, v0 = spread_shift(own[0:24], HALO)
                c1, v1 = spread_shift(own[24:48], HALO + 1)
                c2, v2 = spread_shift(own[48:64], HALO + 2)
                c3, v3 = spread_shift(own[64:72], HALO + 3)
                here = c0 + c1 + jnp.concatenate([c2, zeros8], 0) + jnp.concatenate([c3, zeros16], 0)
                nloc[2 * p + b] = here + carry
                carry = v0 + v1 + jnp.concatenate([v2, zeros8], 0) + jnp.concatenate([v3, zeros16], 0)
        return carry

    nloc[BLOCKS] = lax.fori_loop(0, BLOCKS // UNROLL, normal_step, jnp.zeros((24, 128), F32))
    mate = (src, x * 2 + (core + 1) % 2)
    nhalf_copy = send(nloc.at[pl.ds(32 * ((core + 1) % 2), HALF)], nhalf, nh_s, nh_r, mate)

    for copy in mom_copies:
        copy.wait_recv()
    whole = mom[ccd]
    for k in range(7):
        whole = whole + momr[k]
    solved = solve_rows(lambda r: whole[r : r + 1])
    par[ccd] = jnp.concatenate(solved + [jnp.zeros((3, 128), F32)], 0)
    for k in (4, 5, 3, 2, 6, 7, 1):
        send(par.at[ccd], par.at[ccd], pa_s.at[k - 1], pa_r.at[k - 1], (src, (ccd + k) % 8))
    def pack(halo):
        near = jnp.where(lane < 32, pltpu.roll(halo[1], 16, 1), pltpu.roll(halo[2], 32, 1))
        return jnp.where(lane < 16, halo[0], near)

    nhalf_copy.wait_recv()
    for i in range(16):
        for t in range(2):
            tile = nloc[32 * core + 2 * i + t] + nhalf[2 * i + t]
            for g in range(3):
                nsum[i, 3 * t + g] = tile[8 * g : 8 * g + 8]
        if i:
            nsum[i - 1, 6] = pack([nsum[i, g] for g in range(3)])
    tile = nloc[32 * core + 32] + nhalf[32]
    nsum[15, 6] = pack([tile[8 * g : 8 * g + 8] for g in range(3)])

    def to_owner(i):
        ky, kx = steps16[i]
        there = ((y + ky) % 4) * 4 + (x + kx) % 4
        return send(nsum.at[there], nr.at[i], np_s.at[i], np_r.at[i], plane(ky, kx, 0))

    n_copies = [to_owner(i) for i in range(15)]

    for k in range(1, 8):
        sender = (ccd + 8 - k) % 8
        pltpu.make_async_remote_copy(
            src_ref=par.at[sender], dst_ref=par.at[sender], send_sem=pa_s.at[k - 1], recv_sem=pa_r.at[k - 1],
            device_id=(src, sender), device_id_type=MESH,
        ).wait_recv()
    table = jnp.concatenate([jnp.concatenate([par[2 * h], par[2 * h + 1]], 1) for h in range(4)], 0)
    table = jnp.concatenate(parts(table, 3), 0).astype(BF16)
    upper = sub < 4

    def residual_step(t, carry):
        for part in range(UNROLL // 8):
            window = otlo[:, pl.ds(pl.multiple_of(t * UNROLL * 128 + part * 1024, 1024), 1024)]
            picked = lax.dot_general(table, window, NN, preferred_element_type=F32)
            picked = picked[0:32] + picked[32:64] + picked[64:96]
            for pair in range(4):
                halves = []
                p = t * (UNROLL // 2) + part * 4 + pair
                for b in range(2):
                    d = 2 * p + b
                    high = jnp.broadcast_to(sidx[pl.ds(d, 1), :] >> 8, (8, 128))
                    own = picked[:, pair * 256 + b * 128 : pair * 256 + b * 128 + 128]
                    chosen = own[0:8]
                    for h in range(1, 4):
                        chosen = jnp.where(high == h, own[8 * h : 8 * h + 8], chosen)
                    fitted = jnp.sum(chosen[0:5] * design[:, cols(d)], 0, keepdims=True)
                    r = jnp.where(lane1 < cnt[0, d], obs[pl.ds(d, 1), :] - fitted, 0.0)
                    resid[pl.ds(d, 1), :] = r
                    wr = jnp.broadcast_to(wl[pl.ds(d, 1), :] * r, (8, 128))
                    a = ax8[:, cols(d)] * wr
                    pair01 = a * jnp.where(upper, bb[0, pl.ds(d, 1), :], bb[1, pl.ds(d, 1), :])
                    pair23 = a * jnp.where(upper, bb[2, pl.ds(d, 1), :], bb[3, pl.ds(d, 1), :])
                    stacked = jnp.concatenate([pair01, pair23], 0)
                    halves.append(jnp.concatenate(parts(stacked, 3), 0).astype(BF16))
                both = jnp.concatenate(halves, 1)
                sums = lax.dot_general(both, otk[p], NT, preferred_element_type=F32)
                sums = sums[0:16] + sums[16:32] + sums[32:48]
                for b in range(2):
                    here = carry
                    over = jnp.zeros((8, 128), F32)
                    for g in range(2):
                        value = sums[8 * g : 8 * g + 8, b * 128 : b * 128 + 128]
                        first, second = HALO + 2 * g, HALO + 2 * g + 1
                        turned = jnp.where(upper, pltpu.roll(value, first, 1), pltpu.roll(value, second, 1))
                        limit = jnp.where(upper, first, second)
                        here = here + jnp.where(lane >= limit, turned, 0.0)
                        over = over + jnp.where(lane < limit, turned, 0.0)
                    folded = here + pltpu.roll(here, 4, 0)
                    rloc[2 * p + b] = folded[0:4]
                    carry = over
        return carry

    last = lax.fori_loop(0, BLOCKS // UNROLL, residual_step, jnp.zeros((8, 128), F32))
    last = last + pltpu.roll(last, 4, 0)
    rloc[BLOCKS] = last[0:4]

    rhalf_copy = send(rloc.at[pl.ds(32 * ((core + 1) % 2), HALF)], rhalf, rh_s, rh_r, mate)
    for c in range(8):
        params_o[:, c * 128 : (c + 1) * 128] = par[c, 0:5]
    params_out = pltpu.make_async_copy(params_o, params_h, out_sem.at[0])
    params_out.start()
    rhalf_copy.wait_recv()
    for i in range(16):
        for t in range(2):
            rsum[i, t] = rloc[32 * core + 2 * i + t] + rhalf[2 * i + t]
        rsum[i, 2] = rloc[32 * core + 2 * i + 2] + rhalf[2 * i + 2]
    r_copies = []
    for i, (ky, kx) in enumerate(steps16):
        there = ((y + ky) % 4) * 4 + (x + kx) % 4
        r_copies.append(send(rsum.at[there], rr.at[i], rp_s.at[i], rp_r.at[i], plane(ky, kx, 0)))

    for copy in n_copies:
        copy.wait_recv()
    for g in range(7):
        total = nsum[chip, g]
        for i in range(15):
            total = total + nr[i, g]
        npc[g] = total
    owners = [(16 * g) // 7 for g in range(7)]
    mine = (7 * z + 15) // 16
    is_owner = (16 * mine) // 7 == z
    for g, owner in enumerate(owners):
        step = (owner + 16 - z) % 16

        @pl.when(owner != z)
        def _(g=g, owner=owner, step=step):
            pltpu.make_async_remote_copy(
                src_ref=npc.at[g], dst_ref=nz.at[step - 1], send_sem=nz_s.at[g], recv_sem=nz_r.at[step - 1],
                device_id=(owner * 4 + y, ccd), device_id_type=MESH,
            ).start()

    for copy in r_copies:
        copy.wait_recv()
    rows = []
    for t in range(3):
        total = rsum[chip, t]
        for i in range(15):
            total = total + rr[i, t]
        rows.append(total)
    low = jnp.concatenate(rows[:2], 0)
    edge = jnp.where(lane1 < 16, rows[2][0:1], jnp.where(lane1 < 32, pltpu.roll(rows[2], 16, 1)[1:2], pltpu.roll(rows[2], 32, 1)[2:3]))
    rpc[...] = jnp.where((sub == 3) | (sub == 7), jnp.broadcast_to(edge, (8, 128)), low)
    rz_copies = []
    for kz in zsteps:
        rz_copies.append(send(rpc, rz.at[kz - 1], rz_s.at[kz - 1], rz_r.at[kz - 1], along(kz)))

    @pl.when(is_owner)
    def _():
        total = npc[mine]
        for k in range(15):
            pltpu.make_async_remote_copy(
                src_ref=npc.at[0], dst_ref=nz.at[k], send_sem=nz_s.at[0], recv_sem=nz_r.at[k],
                device_id=along(k + 1), device_id_type=MESH,
            ).wait_recv()
            total = total + nz[k]
        nf[mine] = total
        for k in zsteps:
            pltpu.make_async_remote_copy(
                src_ref=nf.at[mine], dst_ref=nf.at[mine], send_sem=ng_s.at[k - 1], recv_sem=ng_r.at[mine],
                device_id=along(k), device_id_type=MESH,
            ).start()

    for copy in rz_copies:
        copy.wait_recv()
    flat = rpc[...]
    for i in range(15):
        flat = flat + rz[i]
    for g, owner in enumerate(owners):

        @pl.when(owner != z)
        def _(g=g, owner=owner):
            pltpu.make_async_remote_copy(
                src_ref=nf.at[g], dst_ref=nf.at[g], send_sem=ng_s.at[0], recv_sem=ng_r.at[g],
                device_id=(owner * 4 + y, ccd), device_id_type=MESH,
            ).wait_recv()

    def wide(pieces):
        return jnp.concatenate([jnp.broadcast_to(piece, (8, 128)) for piece in pieces], 1)

    edges = [nf[6], pltpu.roll(nf[6], 112, 1), pltpu.roll(nf[6], 96, 1)]

    def band(o, pair):
        g, s = (o, pair) if o < 3 else (pair // 2, 6 + pair % 2)
        return wide([nf[g, s : s + 1], nf[3 + g, s : s + 1], edges[g][s : s + 1]])

    bands = [{} for _ in range(4)]
    for o in range(4):
        for p, (a, b) in enumerate(PAIRS):
            bands[o][a, b] = bands[o][b, a] = band(o, p)
    inside = lax.broadcasted_iota(jnp.int32, (8, 384), 1) < jnp.minimum(KNOTS + HALO - 256 * pid, 256 + 2 * HALO)
    shifted = [flat, pltpu.roll(flat, 112, 1), pltpu.roll(flat, 96, 1)]
    rhs = [wide([flat[i : i + 1], flat[4 + i : 5 + i], shifted[i][3:4]]) for i in range(3)]
    scale = [RELAX / (ATT_RIDGE + bands[0][i, i]) for i in range(3)]
    coef = [jnp.where(inside, rhs[i] * scale[i], 0.0) for i in range(3)]
    for _ in range(1, SWEEPS):
        ahead = [[pltpu.roll(coef[i], 384 - o, 1) for i in range(3)] for o in range(1, 4)]
        fresh = []
        for i in range(3):
            product = coef[i] * ATT_RIDGE
            for k in range(3):
                product = product + bands[0][i, k] * coef[k]
            for o in range(1, 4):
                back = bands[o][i, 0] * coef[0] + bands[o][i, 1] * coef[1] + bands[o][i, 2] * coef[2]
                product = product + pltpu.roll(back, o, 1)
                for k in range(3):
                    product = product + bands[o][i, k] * ahead[o - 1][k]
            fresh.append(jnp.where(inside, coef[i] + scale[i] * (rhs[i] - product), 0.0))
        coef = fresh
    cp[:, 3:4, :] = jnp.zeros((2, 1, 128), F32)
    for i in range(3):
        moved = pltpu.roll(coef[i], 384 - HALO, 1)
        for t in range(2):
            cp[t, i : i + 1] = moved[0:1, t * 128 : (t + 1) * 128]
    for i, k in enumerate(steps32):
        send(cp, cb.at[pl.ds(2 * pid, 2)], cg_s.at[i], cg_r.at[i], plane(*k))
    for t in range(2):
        cb[2 * pid + t] = cp[t]
    cb[BLOCKS] = jnp.zeros((4, 128), F32)
    for i, (ky, kx, kc) in enumerate(steps32):
        sy, sx, sc = (y + 4 - ky) % 4, (x + 4 - kx) % 4, (core + 2 - kc) % 2
        slot = cb.at[pl.ds(2 * (sc * 16 + sy * 4 + sx), 2)]
        pltpu.make_async_remote_copy(
            src_ref=cp, dst_ref=slot, send_sem=cg_s.at[i], recv_sem=cg_r.at[i],
            device_id=(z * 4 + sy, sx * 2 + sc), device_id_type=MESH,
        ).wait_recv()
    att_o[...] = cb[src][0:3]
    att_out = pltpu.make_async_copy(att_o, att_h, out_sem.at[1])
    att_out.start()

    def final_step(t, carry):
        for pair in range(UNROLL // 2):
            p = t * (UNROLL // 2) + pair
            halves = []
            for b in range(2):
                d = 2 * p + b
                now = jnp.concatenate([cb[d], cb[d + 1]], 0)
                turned = [now] + [pltpu.roll(now, 128 - j, 1) for j in range(1, 4)]
                flip = [pltpu.roll(v, 4, 0) for v in turned]
                pair01 = jnp.where(
                    upper, now, jnp.where(lane < 127, flip[1], turned[1])
                )
                pair23 = jnp.where(
                    upper,
                    jnp.where(lane < 126, turned[2], flip[2]),
                    jnp.where(lane < 125, flip[3], turned[3]),
                )
                stacked = jnp.concatenate([pair01, pair23], 0)
                halves.append(jnp.concatenate(parts(stacked, 3), 0).astype(BF16))
            both = jnp.concatenate(halves, 1)
            picked = lax.dot_general(both, otk[p], NN, preferred_element_type=F32)
            picked = picked[0:16] + picked[16:32] + picked[32:48]
            for b in range(2):
                d = 2 * p + b
                own = picked[:, b * 128 : b * 128 + 128]
                b01 = jnp.where(upper, bb[0, pl.ds(d, 1), :], bb[1, pl.ds(d, 1), :])
                b23 = jnp.where(upper, bb[2, pl.ds(d, 1), :], bb[3, pl.ds(d, 1), :])
                terms = ax8[:, cols(d)] * (own[0:8] * b01 + own[8:16] * b23)
                predicted = jnp.sum(terms, 0, keepdims=True)
                res_o[pl.ds(d, 1), :] = jnp.where(
                    lane1 < cnt[0, d], resid[pl.ds(d, 1), :] - predicted, 0.0
                )
        return carry

    lax.fori_loop(0, BLOCKS // UNROLL, final_step, 0)
    res_out = pltpu.make_async_copy(res_o, res_h, out_sem.at[2])
    res_out.start()

    for copy in started:
        copy.wait_send()
    for g, owner in enumerate(owners):

        @pl.when(owner != z)
        def _(g=g, owner=owner):
            pltpu.make_async_remote_copy(
                src_ref=npc.at[g], dst_ref=nz.at[0], send_sem=nz_s.at[g], recv_sem=nz_r.at[0],
                device_id=(owner * 4 + y, ccd), device_id_type=MESH,
            ).wait_send()

    @pl.when(is_owner)
    def _():
        for k in zsteps:
            pltpu.make_async_remote_copy(
                src_ref=nf.at[mine], dst_ref=nf.at[mine], send_sem=ng_s.at[k - 1], recv_sem=ng_r.at[mine],
                device_id=along(k), device_id_type=MESH,
            ).wait_send()

    for copy in (params_out, att_out, res_out):
        copy.wait()


def write_out(params_i, att_i, res_i, params_o, att_o, res_o, params, attitude, residual, sems):
    held = (params, attitude, residual)
    inward = [pltpu.make_async_copy(a, b, sems.at[i]) for i, (a, b) in enumerate(zip((params_i, att_i, res_i), held))]
    outward = [pltpu.make_async_copy(a, b, sems.at[i + 3]) for i, (a, b) in enumerate(zip(held, (params_o, att_o, res_o)))]
    for copy in inward:
        copy.start()
    for there, back in zip(inward, outward):
        there.wait()
        back.start()
    for copy in outward:
        copy.wait()


def on_device(design, observed, weight, phase_frac, axis_factors, source_index, knot_index, counts):
    dma = pltpu.SemaphoreType.DMA
    vm = lambda *shape: pltpu.VMEM(shape, F32)
    square = lambda v: v.reshape(64, 128)
    params, attitude, residual = pl.pallas_call(
        kernel,
        out_shape=(
            jax.ShapeDtypeStruct((5, 1024), F32),
            jax.ShapeDtypeStruct((3, 128), F32),
            jax.ShapeDtypeStruct((64, 128), F32),
        ),
        in_specs=[pl.BlockSpec(memory_space=pl.ANY)] * 8,
        out_specs=(pl.BlockSpec(memory_space=pl.ANY),) * 3,
        scratch_shapes=[
            vm(5, 1024), vm(3, 128), vm(64, 128), dma((3,)),
            vm(5, 8192), vm(64, 128), vm(64, 128), vm(64, 128), vm(3, 8192),
            pltpu.VMEM((64, 128), jnp.int32), pltpu.VMEM((64, 128), jnp.int32), pltpu.SMEM((1, 64), jnp.int32), dma((8,)),
            pltpu.VMEM((256, 8192), BF16),
            pltpu.VMEM((32, 256, 256), BF16),
            vm(14, 64, 128), vm(64, 128), vm(8, 8192),
            pltpu.VMEM((UNROLL // 8, 256, 1024), BF16),
            vm(256, 256), vm(8, 24, 128), vm(7, 24, 128), vm(8, 8, 128),
            vm(TILES, 24, 128), vm(HALF, 24, 128), vm(16, 7, 8, 128), vm(15, 7, 8, 128),
            vm(7, 8, 128), vm(15, 8, 128), vm(7, 8, 128),
            vm(TILES, 4, 128), vm(HALF, 4, 128), vm(16, 3, 4, 128), vm(15, 3, 4, 128),
            vm(8, 128), vm(15, 8, 128), vm(2, 4, 128), vm(TILES, 4, 128), vm(64, 128),
            dma((7,)), dma((7,)), dma((7,)), dma((7,)),
            dma, dma, dma((15,)), dma((15,)), dma((7,)), dma((15,)), dma((15,)), dma((7,)),
            dma, dma, dma((15,)), dma((15,)), dma((15,)), dma((15,)), dma((31,)), dma((31,)),
        ],
        compiler_params=pltpu.CompilerParams(
            collective_id=0, has_side_effects=True, vmem_limit_bytes=60 * 1024 * 1024
        ),
    )(
        design, square(observed), square(weight), square(phase_frac), axis_factors,
        square(source_index), square(knot_index), counts.reshape(1, 64),
    )
    anywhere = pl.BlockSpec(memory_space=pl.ANY)
    params, attitude, residual = pl.pallas_call(
        write_out,
        out_shape=(
            jax.ShapeDtypeStruct((5, 1024), F32),
            jax.ShapeDtypeStruct((3, 128), F32),
            jax.ShapeDtypeStruct((64, 128), F32),
        ),
        in_specs=[anywhere] * 3,
        out_specs=(anywhere,) * 3,
        scratch_shapes=[vm(5, 1024), vm(3, 128), vm(64, 128), dma((6,))],
        compiler_params=pltpu.CompilerParams(vmem_limit_bytes=60 * 1024 * 1024),
    )(params, attitude, residual)
    return params, attitude, residual.reshape(8192)


def solution(mesh):
    rows = P(("src", "ccd"))
    wide = P(None, ("src", "ccd"))
    in_specs = (wide, rows, rows, rows, wide, rows, rows, P("src", "ccd", None))
    out_specs = (P(None, "src"), P(None, "src"), rows)
    return jax.shard_map(on_device, mesh=mesh, in_specs=in_specs, out_specs=out_specs, check_vma=False)
```

time: 67.6 us -> 54.9 us (0.81)
  local copies, waits for them, and re-layouts: 8.1 us -> 0 us
  Pallas kernels: 58.3 us -> 54 us
    unnamed x19 -> x0, local copies, waits for them, and re-layouts: 8.1 us -> none
    pallas_call x1, Pallas kernels: 58.3 us -> 52.6 us  [on_device(): pl.pallas_call(kernel, out_shape=(jax.ShapeDtypeStruct((5, 1024), F32), j...]
    pallas_call x0 -> x1, Pallas kernels: none -> 1.45 us  [on_device(): pl.pallas_call(write_out, out_shape=(jax.ShapeDtypeStruct((5, 1024), F32)...]
where the time goes in v2:
time: 54.9 us; the launch traced here: 54.7 us
  Pallas kernels  54 us (98%)
  between operations  0.64 us (1%)
    pallas_call x1, Pallas kernels, on_device(): pl.pallas_call(kernel, out_shape=(jax.ShapeDtypeStruct((5, 1024), F32), j...  52.6 us
    pallas_call x1, Pallas kernels, on_device(): pl.pallas_call(write_out, out_shape=(jax.ShapeDtypeStruct((5, 1024), F32)...  1.45 us

profile of v2, /device:TPU:1, one launch (start us, length us, event | category | flops | bytes accessed | tf_op | source)
XLA Modules:
  0.0 54.7 jit_solution(6164708905309381013)
XLA Ops:
  0.6 52.6 %shard_map.103 = (f32[5,1024]{1,0:T(8,128)}, f32[3,128]{1,0:T(4,128)}, f32[64,128]{1,0:T(8,128)}) custom-call(f32[5,8192]{1,0:T(8,128)} %design_h.1, f32[64,128]{1,0:T(8,128)} %bitcast.7, f32[64,128]{1,0:T(8,128)} %bitcast.8, f32[64,128]{1,0:T(8,128)} %bitcast.9, f32[3,8192]{1,0:T(4,128)} %ax_h.1, s32[64,128]{1,0:T(8,128)} %bitcast.10, s32[64,128]{1,0:T(8,128)} %bitcast.11, ...), custom_call_target="tpu_custom_call" | custom-call | tf_op jit(solution)/shard_map/pallas_call | solution.py:563
  53.2 1.4 %shard_map.104 = (f32[5,1024]{1,0:T(8,128)}, f32[3,128]{1,0:T(4,128)}, f32[64,128]{1,0:T(8,128)}) custom-call(f32[5,1024]{1,0:T(8,128)} %get-tuple-element.9.params_i, f32[3,128]{1,0:T(4,128)} %get-tuple-element.10.att_i, f32[64,128]{1,0:T(8,128)} %get-tuple-element.11.res_i), custom_call_target="tpu_custom_call" | custom-call | tf_op jit(solution)/shard_map/pallas_call | solution.py:597

commit v3 on v2

--- a/solution.py
+++ b/solution.py
@@ -20,6 +20,7 @@
 KNOTS = 8192
 HALO = 6
 UNROLL = 16
+LONG = 32
 PAIRS = [(0, 0), (0, 1), (0, 2), (1, 1), (1, 2), (2, 2)]
 NT = (((1,), (1,)), ((), ()))
 NN = (((1,), (0,)), ((), ()))
@@ -73,7 +74,7 @@
     params_h, att_h, res_h,
     params_o, att_o, res_o, out_sem,
     design, obs, wt, ph, ax, sidx, kidx, cnt, in_sem,
-    otlo, otk, bb, wl, ax8, lhs, acc, mom, momr, par,
+    otlo, otk, bb, wl, ax8, acc, mom, momr, par,
     nloc, nhalf, nsum, nr, npc, nz, nf,
     rloc, rhalf, rsum, rr, rpc, rz, cp, cb, resid,
     ma_s, ma_r, pa_s, pa_r, nh_s, nh_r, np_s, np_r, nz_s, nz_r, ng_s, ng_r,
@@ -95,7 +96,6 @@
     steps16 = [(2, 2), (2, 1), (2, 3), (1, 2), (3, 2), (2, 0), (0, 2), (1, 1), (3, 3), (1, 3), (3, 1), (1, 0), (3, 0), (0, 1), (0, 3)]
     steps32 = [(ky, kx, kc) for ky, kx in steps16 for kc in (1, 0)] + [(0, 0, 1)]
     zsteps = [8, 7, 9, 6, 10, 5, 11, 4, 12, 3, 13, 2, 14, 1, 15]
-    started = []
 
     loads = []
     held = (sidx, wt, design, obs, ph, ax, kidx)
@@ -111,8 +111,9 @@
             src_ref=a, dst_ref=b, send_sem=ssem, recv_sem=rsem, device_id=to, device_id_type=MESH
         )
         copy.start()
-        started.append(copy)
-        return copy
+
+    def settle(ref, sem):
+        pltpu.make_async_copy(ref, ref, sem).wait()
 
     barrier = pltpu.get_barrier_semaphore()
     for k in steps32:
@@ -125,7 +126,6 @@
     sub = lax.broadcasted_iota(jnp.int32, (8, 128), 0)
     iota256 = lax.broadcasted_iota(jnp.int32, (256, 128), 0).astype(F32).astype(BF16)
     one, zero = jnp.ones((256, 128), BF16), jnp.zeros((256, 128), BF16)
-    nought = jnp.zeros((64, 128), BF16)
 
     def cols(d):
         return pl.ds(pl.multiple_of(d * 128, 128), 128)
@@ -134,8 +134,11 @@
         packed = jnp.broadcast_to(row.astype(F32), (16, 128)).astype(BF16)
         return jnp.concatenate([packed] * count, 0)
 
-    def hot(row):
-        return jnp.where(iota256 == tall(row, 16), one, zero)
+    def hot(row, size):
+        return jnp.where(iota256[:size] == tall(row, size // 16), one[:size], zero[:size])
+
+    def dot(a, b, dims):
+        return lax.dot_general(a, b, dims, precision=lax.Precision.DEFAULT, preferred_element_type=F32)
 
     for copy in loads[:5]:
         copy.wait()
@@ -144,10 +147,12 @@
     def moments_step(t, carry):
         total = None
         for part in range(UNROLL // 8):
+            lefts, hots = [], []
             for b in range(8):
                 d = t * UNROLL + part * 8 + b
                 s_row = sidx[pl.ds(d, 1), :]
-                otlo[:, cols(d)] = hot(s_row & 255)
+                hots.append(hot(s_row & 255, 256))
+                otlo[:, cols(d)] = hots[-1]
                 high = tall(s_row >> 8, 4)
                 w = jnp.where(lane1 < cnt[0, d], wt[pl.ds(d, 1), :], 0.0)
                 wl[pl.ds(d, 1), :] = w
@@ -163,11 +168,9 @@
                 gc = parts(w * ec * e2, 3)
                 rows = [ga[0], gb[0], ga[1], gb[1], ga[2], gb[2], jnp.where(sub < 4, gc[0], gc[1]), gc[2]]
                 stacked = jnp.concatenate(rows, 0).astype(BF16)
-                for h in range(4):
-                    masked = jnp.where(high == jnp.full((64, 128), h, BF16), stacked, nought)
-                    lhs[part, 64 * h : 64 * h + 64, b * 128 : b * 128 + 128] = masked
-            window = otlo[:, pl.ds(pl.multiple_of(t * UNROLL * 128 + part * 1024, 1024), 1024)]
-            product = lax.dot_general(lhs[part], window, NT, preferred_element_type=F32)
+                masked = [jnp.where(high == jnp.full((64, 128), h, BF16), stacked, zero[:64]) for h in range(4)]
+                lefts.append(jnp.concatenate(masked, 0))
+            product = dot(jnp.concatenate(lefts, 1), jnp.concatenate(hots, 1), NT)
             total = product if total is None else total + product
         acc[...] += total
         return carry
@@ -180,10 +183,9 @@
         mom[2 * h] = total[:, :128]
         mom[2 * h + 1] = total[:, 128:]
     pl.semaphore_wait(barrier, len(steps32) + len(zsteps))
-    mom_copies = []
     for k in (4, 5, 3, 2, 6, 7, 1):
         to = (ccd + k) % 8
-        mom_copies.append(send(mom.at[to], momr.at[k - 1], ma_s.at[k - 1], ma_r.at[k - 1], (src, to)))
+        send(mom.at[to], momr.at[k - 1], ma_s, ma_r, (src, to))
 
     for copy in loads[5:]:
         copy.wait()
@@ -217,10 +219,11 @@
     def normal_step(t, carry):
         for pair in range(UNROLL // 2):
             p = t * (UNROLL // 2) + pair
-            halves = []
+            halves, hots = [], []
             for b in range(2):
                 d = 2 * p + b
-                otk[p, :, b * 128 : b * 128 + 128] = hot(kidx[pl.ds(d, 1), :] + 128 * b)
+                own = hot(kidx[pl.ds(d, 1), :], 128)
+                hots.append(jnp.concatenate([own, zero[:128]] if b == 0 else [zero[:128], own], 0))
                 w = wl[pl.ds(d, 1), :]
                 a = [jnp.broadcast_to(ax[i : i + 1, cols(d)], (8, 128)) for i in range(3)]
                 wa = [w * a[i] for i in range(3)]
@@ -243,7 +246,9 @@
                 stacked = jnp.concatenate(groups, 0)
                 halves.append(jnp.concatenate(parts(stacked, 2), 0).astype(BF16))
             both = jnp.concatenate(halves, 1)
-            sums = lax.dot_general(both, otk[p], NT, preferred_element_type=F32)
+            hot2 = jnp.concatenate(hots, 1)
+            otk[p] = hot2
+            sums = dot(both, hot2, NT)
             sums = sums[:72] + sums[72:]
             zeros8 = jnp.zeros((8, 128), F32)
             zeros16 = jnp.zeros((16, 128), F32)
@@ -260,22 +265,21 @@
 
     nloc[BLOCKS] = lax.fori_loop(0, BLOCKS // UNROLL, normal_step, jnp.zeros((24, 128), F32))
     mate = (src, x * 2 + (core + 1) % 2)
-    nhalf_copy = send(nloc.at[pl.ds(32 * ((core + 1) % 2), HALF)], nhalf, nh_s, nh_r, mate)
-
-    for copy in mom_copies:
-        copy.wait_recv()
+    send(nloc.at[pl.ds(32 * ((core + 1) % 2), HALF)], nhalf, nh_s, nh_r, mate)
+
+    settle(momr, ma_r)
     whole = mom[ccd]
     for k in range(7):
         whole = whole + momr[k]
     solved = solve_rows(lambda r: whole[r : r + 1])
     par[ccd] = jnp.concatenate(solved + [jnp.zeros((3, 128), F32)], 0)
     for k in (4, 5, 3, 2, 6, 7, 1):
-        send(par.at[ccd], par.at[ccd], pa_s.at[k - 1], pa_r.at[k - 1], (src, (ccd + k) % 8))
+        send(par.at[ccd], par.at[ccd], pa_s, pa_r, (src, (ccd + k) % 8))
     def pack(halo):
         near = jnp.where(lane < 32, pltpu.roll(halo[1], 16, 1), pltpu.roll(halo[2], 32, 1))
         return jnp.where(lane < 16, halo[0], near)
 
-    nhalf_copy.wait_recv()
+    settle(nhalf, nh_r)
     for i in range(16):
         for t in range(2):
             tile = nloc[32 * core + 2 * i + t] + nhalf[2 * i + t]
@@ -289,28 +293,24 @@
     def to_owner(i):
         ky, kx = steps16[i]
         there = ((y + ky) % 4) * 4 + (x + kx) % 4
-        return send(nsum.at[there], nr.at[i], np_s.at[i], np_r.at[i], plane(ky, kx, 0))
-
-    n_copies = [to_owner(i) for i in range(15)]
-
-    for k in range(1, 8):
-        sender = (ccd + 8 - k) % 8
-        pltpu.make_async_remote_copy(
-            src_ref=par.at[sender], dst_ref=par.at[sender], send_sem=pa_s.at[k - 1], recv_sem=pa_r.at[k - 1],
-            device_id=(src, sender), device_id_type=MESH,
-        ).wait_recv()
+        send(nsum.at[there], nr.at[i], np_s, np_r, plane(ky, kx, 0))
+
+    for i in range(15):
+        to_owner(i)
+
+    settle(par.at[0:7], pa_r)
     table = jnp.concatenate([jnp.concatenate([par[2 * h], par[2 * h + 1]], 1) for h in range(4)], 0)
     table = jnp.concatenate(parts(table, 3), 0).astype(BF16)
     upper = sub < 4
 
     def residual_step(t, carry):
-        for part in range(UNROLL // 8):
-            window = otlo[:, pl.ds(pl.multiple_of(t * UNROLL * 128 + part * 1024, 1024), 1024)]
-            picked = lax.dot_general(table, window, NN, preferred_element_type=F32)
+        for part in range(LONG // 8):
+            window = otlo[:, pl.ds(pl.multiple_of(t * LONG * 128 + part * 1024, 1024), 1024)]
+            picked = dot(table, window, NN)
             picked = picked[0:32] + picked[32:64] + picked[64:96]
             for pair in range(4):
                 halves = []
-                p = t * (UNROLL // 2) + part * 4 + pair
+                p = t * (LONG // 2) + part * 4 + pair
                 for b in range(2):
                     d = 2 * p + b
                     high = jnp.broadcast_to(sidx[pl.ds(d, 1), :] >> 8, (8, 128))
@@ -328,7 +328,7 @@
                     stacked = jnp.concatenate([pair01, pair23], 0)
                     halves.append(jnp.concatenate(parts(stacked, 3), 0).astype(BF16))
                 both = jnp.concatenate(halves, 1)
-                sums = lax.dot_general(both, otk[p], NT, preferred_element_type=F32)
+                sums = dot(both, otk[p], NT)
                 sums = sums[0:16] + sums[16:32] + sums[32:48]
                 for b in range(2):
                     here = carry
@@ -345,27 +345,25 @@
                     carry = over
         return carry
 
-    last = lax.fori_loop(0, BLOCKS // UNROLL, residual_step, jnp.zeros((8, 128), F32))
+    last = lax.fori_loop(0, BLOCKS // LONG, residual_step, jnp.zeros((8, 128), F32))
     last = last + pltpu.roll(last, 4, 0)
     rloc[BLOCKS] = last[0:4]
 
-    rhalf_copy = send(rloc.at[pl.ds(32 * ((core + 1) % 2), HALF)], rhalf, rh_s, rh_r, mate)
+    send(rloc.at[pl.ds(32 * ((core + 1) % 2), HALF)], rhalf, rh_s, rh_r, mate)
     for c in range(8):
         params_o[:, c * 128 : (c + 1) * 128] = par[c, 0:5]
     params_out = pltpu.make_async_copy(params_o, params_h, out_sem.at[0])
     params_out.start()
-    rhalf_copy.wait_recv()
+    settle(rhalf, rh_r)
     for i in range(16):
         for t in range(2):
             rsum[i, t] = rloc[32 * core + 2 * i + t] + rhalf[2 * i + t]
         rsum[i, 2] = rloc[32 * core + 2 * i + 2] + rhalf[2 * i + 2]
-    r_copies = []
     for i, (ky, kx) in enumerate(steps16):
         there = ((y + ky) % 4) * 4 + (x + kx) % 4
-        r_copies.append(send(rsum.at[there], rr.at[i], rp_s.at[i], rp_r.at[i], plane(ky, kx, 0)))
-
-    for copy in n_copies:
-        copy.wait_recv()
+        send(rsum.at[there], rr.at[i], rp_s, rp_r, plane(ky, kx, 0))
+
+    settle(nr, np_r)
     for g in range(7):
         total = nsum[chip, g]
         for i in range(15):
@@ -380,12 +378,11 @@
         @pl.when(owner != z)
         def _(g=g, owner=owner, step=step):
             pltpu.make_async_remote_copy(
-                src_ref=npc.at[g], dst_ref=nz.at[step - 1], send_sem=nz_s.at[g], recv_sem=nz_r.at[step - 1],
+                src_ref=npc.at[g], dst_ref=nz.at[step - 1], send_sem=nz_s, recv_sem=nz_r,
                 device_id=(owner * 4 + y, ccd), device_id_type=MESH,
             ).start()
 
-    for copy in r_copies:
-        copy.wait_recv()
+    settle(rr, rp_r)
     rows = []
     for t in range(3):
         total = rsum[chip, t]
@@ -395,39 +392,33 @@
     low = jnp.concatenate(rows[:2], 0)
     edge = jnp.where(lane1 < 16, rows[2][0:1], jnp.where(lane1 < 32, pltpu.roll(rows[2], 16, 1)[1:2], pltpu.roll(rows[2], 32, 1)[2:3]))
     rpc[...] = jnp.where((sub == 3) | (sub == 7), jnp.broadcast_to(edge, (8, 128)), low)
-    rz_copies = []
     for kz in zsteps:
-        rz_copies.append(send(rpc, rz.at[kz - 1], rz_s.at[kz - 1], rz_r.at[kz - 1], along(kz)))
+        send(rpc, rz.at[kz - 1], rz_s, rz_r, along(kz))
 
     @pl.when(is_owner)
     def _():
         total = npc[mine]
+        settle(nz, nz_r)
         for k in range(15):
-            pltpu.make_async_remote_copy(
-                src_ref=npc.at[0], dst_ref=nz.at[k], send_sem=nz_s.at[0], recv_sem=nz_r.at[k],
-                device_id=along(k + 1), device_id_type=MESH,
-            ).wait_recv()
             total = total + nz[k]
         nf[mine] = total
         for k in zsteps:
             pltpu.make_async_remote_copy(
-                src_ref=nf.at[mine], dst_ref=nf.at[mine], send_sem=ng_s.at[k - 1], recv_sem=ng_r.at[mine],
+                src_ref=nf.at[mine], dst_ref=nf.at[mine], send_sem=ng_s, recv_sem=ng_r,
                 device_id=along(k), device_id_type=MESH,
             ).start()
 
-    for copy in rz_copies:
-        copy.wait_recv()
+    settle(rz, rz_r)
     flat = rpc[...]
     for i in range(15):
         flat = flat + rz[i]
-    for g, owner in enumerate(owners):
-
-        @pl.when(owner != z)
-        def _(g=g, owner=owner):
-            pltpu.make_async_remote_copy(
-                src_ref=nf.at[g], dst_ref=nf.at[g], send_sem=ng_s.at[0], recv_sem=ng_r.at[g],
-                device_id=(owner * 4 + y, ccd), device_id_type=MESH,
-            ).wait_recv()
+    @pl.when(is_owner)
+    def _():
+        settle(nf.at[0:6], ng_r)
+
+    @pl.when(jnp.logical_not(is_owner))
+    def _():
+        settle(nf, ng_r)
 
     def wide(pieces):
         return jnp.concatenate([jnp.broadcast_to(piece, (8, 128)) for piece in pieces], 1)
@@ -467,24 +458,18 @@
         for t in range(2):
             cp[t, i : i + 1] = moved[0:1, t * 128 : (t + 1) * 128]
     for i, k in enumerate(steps32):
-        send(cp, cb.at[pl.ds(2 * pid, 2)], cg_s.at[i], cg_r.at[i], plane(*k))
+        send(cp, cb.at[pl.ds(2 * pid, 2)], cg_s, cg_r, plane(*k))
     for t in range(2):
         cb[2 * pid + t] = cp[t]
     cb[BLOCKS] = jnp.zeros((4, 128), F32)
-    for i, (ky, kx, kc) in enumerate(steps32):
-        sy, sx, sc = (y + 4 - ky) % 4, (x + 4 - kx) % 4, (core + 2 - kc) % 2
-        slot = cb.at[pl.ds(2 * (sc * 16 + sy * 4 + sx), 2)]
-        pltpu.make_async_remote_copy(
-            src_ref=cp, dst_ref=slot, send_sem=cg_s.at[i], recv_sem=cg_r.at[i],
-            device_id=(z * 4 + sy, sx * 2 + sc), device_id_type=MESH,
-        ).wait_recv()
+    settle(cb.at[0:62], cg_r)
     att_o[...] = cb[src][0:3]
     att_out = pltpu.make_async_copy(att_o, att_h, out_sem.at[1])
     att_out.start()
 
     def final_step(t, carry):
-        for pair in range(UNROLL // 2):
-            p = t * (UNROLL // 2) + pair
+        for pair in range(LONG // 2):
+            p = t * (LONG // 2) + pair
             halves = []
             for b in range(2):
                 d = 2 * p + b
@@ -502,7 +487,7 @@
                 stacked = jnp.concatenate([pair01, pair23], 0)
                 halves.append(jnp.concatenate(parts(stacked, 3), 0).astype(BF16))
             both = jnp.concatenate(halves, 1)
-            picked = lax.dot_general(both, otk[p], NN, preferred_element_type=F32)
+            picked = dot(both, otk[p], NN)
             picked = picked[0:16] + picked[16:32] + picked[32:48]
             for b in range(2):
                 d = 2 * p + b
@@ -516,28 +501,27 @@
                 )
         return carry
 
-    lax.fori_loop(0, BLOCKS // UNROLL, final_step, 0)
+    lax.fori_loop(0, BLOCKS // LONG, final_step, 0)
     res_out = pltpu.make_async_copy(res_o, res_h, out_sem.at[2])
     res_out.start()
 
-    for copy in started:
-        copy.wait_send()
-    for g, owner in enumerate(owners):
-
-        @pl.when(owner != z)
-        def _(g=g, owner=owner):
-            pltpu.make_async_remote_copy(
-                src_ref=npc.at[g], dst_ref=nz.at[0], send_sem=nz_s.at[g], recv_sem=nz_r.at[0],
-                device_id=(owner * 4 + y, ccd), device_id_type=MESH,
-            ).wait_send()
+    settle(momr, ma_s)
+    settle(par.at[0:7], pa_s)
+    settle(nhalf, nh_s)
+    settle(nr, np_s)
+    settle(rhalf, rh_s)
+    settle(rr, rp_s)
+    settle(rz, rz_s)
+    settle(cb.at[0:62], cg_s)
 
     @pl.when(is_owner)
     def _():
-        for k in zsteps:
-            pltpu.make_async_remote_copy(
-                src_ref=nf.at[mine], dst_ref=nf.at[mine], send_sem=ng_s.at[k - 1], recv_sem=ng_r.at[mine],
-                device_id=along(k), device_id_type=MESH,
-            ).wait_send()
+        settle(nz.at[0:6], nz_s)
+        settle(nz, ng_s)
+
+    @pl.when(jnp.logical_not(is_owner))
+    def _():
+        settle(nz.at[0:7], nz_s)
 
     for copy in (params_out, att_out, res_out):
         copy.wait()
@@ -576,16 +560,13 @@
             pltpu.VMEM((256, 8192), BF16),
             pltpu.VMEM((32, 256, 256), BF16),
             vm(14, 64, 128), vm(64, 128), vm(8, 8192),
-            pltpu.VMEM((UNROLL // 8, 256, 1024), BF16),
             vm(256, 256), vm(8, 24, 128), vm(7, 24, 128), vm(8, 8, 128),
             vm(TILES, 24, 128), vm(HALF, 24, 128), vm(16, 7, 8, 128), vm(15, 7, 8, 128),
             vm(7, 8, 128), vm(15, 8, 128), vm(7, 8, 128),
             vm(TILES, 4, 128), vm(HALF, 4, 128), vm(16, 3, 4, 128), vm(15, 3, 4, 128),
             vm(8, 128), vm(15, 8, 128), vm(2, 4, 128), vm(TILES, 4, 128), vm(64, 128),
-            dma((7,)), dma((7,)), dma((7,)), dma((7,)),
-            dma, dma, dma((15,)), dma((15,)), dma((7,)), dma((15,)), dma((15,)), dma((7,)),
-            dma, dma, dma((15,)), dma((15,)), dma((15,)), dma((15,)), dma((31,)), dma((31,)),
-        ],
+        ]
+        + [dma] * 20,
         compiler_params=pltpu.CompilerParams(
             collective_id=0, has_side_effects=True, vmem_limit_bytes=60 * 1024 * 1024
         ),

time: 54.9 us -> 52.5 us (0.956)
  Pallas kernels: 54 us -> 51.6 us
    pallas_call x1, Pallas kernels: 52.6 us -> 50.2 us  [on_device(): pl.pallas_call(kernel, out_shape=(jax.ShapeDtypeStruct((5, 1024), F32), j...]
where the time goes in v3:
time: 52.5 us; the launch traced here: 52.3 us
  Pallas kernels  51.6 us (98%)
  between operations  0.64 us (1%)
    pallas_call x1, Pallas kernels, on_device(): pl.pallas_call(kernel, out_shape=(jax.ShapeDtypeStruct((5, 1024), F32), j...  50.2 us
    pallas_call x1, Pallas kernels, on_device(): pl.pallas_call(write_out, out_shape=(jax.ShapeDtypeStruct((5, 1024), F32)...  1.45 us

profile of v3, /device:TPU:1, one launch (start us, length us, event | category | flops | bytes accessed | tf_op | source)
XLA Modules:
  0.0 52.3 jit_solution(15659444492429942321)
XLA Ops:
  0.6 50.2 %shard_map.103 = (f32[5,1024]{1,0:T(8,128)}, f32[3,128]{1,0:T(4,128)}, f32[64,128]{1,0:T(8,128)}) custom-call(f32[5,8192]{1,0:T(8,128)} %design_h.1, f32[64,128]{1,0:T(8,128)} %bitcast.7, f32[64,128]{1,0:T(8,128)} %bitcast.8, f32[64,128]{1,0:T(8,128)} %bitcast.9, f32[3,8192]{1,0:T(4,128)} %ax_h.1, s32[64,128]{1,0:T(8,128)} %bitcast.10, s32[64,128]{1,0:T(8,128)} %bitcast.11, ...), custom_call_target="tpu_custom_call" | custom-call | tf_op jit(solution)/shard_map/pallas_call | solution.py:547
  50.8 1.4 %shard_map.104 = (f32[5,1024]{1,0:T(8,128)}, f32[3,128]{1,0:T(4,128)}, f32[64,128]{1,0:T(8,128)}) custom-call(f32[5,1024]{1,0:T(8,128)} %get-tuple-element.9.params_i, f32[3,128]{1,0:T(4,128)} %get-tuple-element.10.att_i, f32[64,128]{1,0:T(8,128)} %get-tuple-element.11.res_i), custom_call_target="tpu_custom_call" | custom-call | tf_op jit(solution)/shard_map/pallas_call | solution.py:578

commit v4 on v3

--- a/solution.py
+++ b/solution.py
@@ -78,7 +78,7 @@
     nloc, nhalf, nsum, nr, npc, nz, nf,
     rloc, rhalf, rsum, rr, rpc, rz, cp, cb, resid,
     ma_s, ma_r, pa_s, pa_r, nh_s, nh_r, np_s, np_r, nz_s, nz_r, ng_s, ng_r,
-    rh_s, rh_r, rp_s, rp_r, rz_s, rz_r, cg_s, cg_r,
+    rh_s, rh_r, rp_s, rp_r, rz_s, rz_r, cg_s, cg_r, from_low, from_high,
 ):
     src = lax.axis_index("src")
     ccd = lax.axis_index("ccd")
@@ -118,8 +118,19 @@
     barrier = pltpu.get_barrier_semaphore()
     for k in steps32:
         pl.semaphore_signal(barrier, inc=1, device_id=plane(*k), device_id_type=MESH)
-    for k in zsteps:
+    for k in (1, 15):
         pl.semaphore_signal(barrier, inc=1, device_id=along(k), device_id_type=MESH)
+
+    def tell():
+        pl.semaphore_signal(from_low, inc=1, device_id=along(1), device_id_type=MESH)
+        pl.semaphore_signal(from_high, inc=1, device_id=along(15), device_id_type=MESH)
+
+    def heard(last=False):
+        pl.semaphore_wait(from_low, 1)
+        pl.semaphore_wait(from_high, 1)
+        if not last:
+            tell()
+
 
     lane = lax.broadcasted_iota(jnp.int32, (8, 128), 1)
     lane1 = lax.broadcasted_iota(jnp.int32, (1, 128), 1)
@@ -146,10 +157,10 @@
 
     def moments_step(t, carry):
         total = None
-        for part in range(UNROLL // 8):
+        for part in range(LONG // 8):
             lefts, hots = [], []
             for b in range(8):
-                d = t * UNROLL + part * 8 + b
+                d = t * LONG + part * 8 + b
                 s_row = sidx[pl.ds(d, 1), :]
                 hots.append(hot(s_row & 255, 256))
                 otlo[:, cols(d)] = hots[-1]
@@ -175,14 +186,15 @@
         acc[...] += total
         return carry
 
-    lax.fori_loop(0, BLOCKS // UNROLL, moments_step, 0)
+    lax.fori_loop(0, BLOCKS // LONG, moments_step, 0)
     for h in range(4):
         v = [acc[64 * h + 8 * i : 64 * h + 8 * i + 8] for i in range(8)]
         tail = v[6] + pltpu.roll(v[6], 4, 0) + v[7]
         total = jnp.concatenate([v[0] + v[2] + v[4], v[1] + v[3] + v[5], tail], 0)
         mom[2 * h] = total[:, :128]
         mom[2 * h + 1] = total[:, 128:]
-    pl.semaphore_wait(barrier, len(steps32) + len(zsteps))
+    pl.semaphore_wait(barrier, len(steps32) + 2)
+    tell()
     for k in (4, 5, 3, 2, 6, 7, 1):
         to = (ccd + k) % 8
         send(mom.at[to], momr.at[k - 1], ma_s, ma_r, (src, to))
@@ -263,10 +275,17 @@
                 carry = v0 + v1 + jnp.concatenate([v2, zeros8], 0) + jnp.concatenate([v3, zeros16], 0)
         return carry
 
-    nloc[BLOCKS] = lax.fori_loop(0, BLOCKS // UNROLL, normal_step, jnp.zeros((24, 128), F32))
     mate = (src, x * 2 + (core + 1) % 2)
+    empty = jnp.zeros((24, 128), F32)
+    nloc[BLOCKS] = empty
+    carried = lax.fori_loop(0, 3, lambda t, c: normal_step(t + 1 - core, c), empty)
+    nloc[64 - 16 * core] = carried
     send(nloc.at[pl.ds(32 * ((core + 1) % 2), HALF)], nhalf, nh_s, nh_r, mate)
-
+    heard()
+    carried = normal_step(3 * core, jnp.where(core == 1, carried, 0.0))
+    nloc[16 + 48 * core] = nloc[16 + 48 * core] + carried
+
+    heard()
     settle(momr, ma_r)
     whole = mom[ccd]
     for k in range(7):
@@ -297,8 +316,10 @@
 
     for i in range(15):
         to_owner(i)
+    heard()
 
     settle(par.at[0:7], pa_r)
+    heard()
     table = jnp.concatenate([jnp.concatenate([par[2 * h], par[2 * h + 1]], 1) for h in range(4)], 0)
     table = jnp.concatenate(parts(table, 3), 0).astype(BF16)
     upper = sub < 4
@@ -350,6 +371,7 @@
     rloc[BLOCKS] = last[0:4]
 
     send(rloc.at[pl.ds(32 * ((core + 1) % 2), HALF)], rhalf, rh_s, rh_r, mate)
+    heard()
     for c in range(8):
         params_o[:, c * 128 : (c + 1) * 128] = par[c, 0:5]
     params_out = pltpu.make_async_copy(params_o, params_h, out_sem.at[0])
@@ -363,12 +385,14 @@
         there = ((y + ky) % 4) * 4 + (x + kx) % 4
         send(rsum.at[there], rr.at[i], rp_s, rp_r, plane(ky, kx, 0))
 
+    heard()
     settle(nr, np_r)
     for g in range(7):
         total = nsum[chip, g]
         for i in range(15):
             total = total + nr[i, g]
         npc[g] = total
+    heard(last=True)
     owners = [(16 * g) // 7 for g in range(7)]
     mine = (7 * z + 15) // 16
     is_owner = (16 * mine) // 7 == z
@@ -566,7 +590,8 @@
             vm(TILES, 4, 128), vm(HALF, 4, 128), vm(16, 3, 4, 128), vm(15, 3, 4, 128),
             vm(8, 128), vm(15, 8, 128), vm(2, 4, 128), vm(TILES, 4, 128), vm(64, 128),
         ]
-        + [dma] * 20,
+        + [dma] * 20
+        + [pltpu.SemaphoreType.REGULAR] * 2,
         compiler_params=pltpu.CompilerParams(
             collective_id=0, has_side_effects=True, vmem_limit_bytes=60 * 1024 * 1024
         ),

time: 52.5 us -> 51.3 us (0.977)
  Pallas kernels: 51.6 us -> 50.4 us
    pallas_call x1, Pallas kernels: 50.2 us -> 49 us  [on_device(): pl.pallas_call(kernel, out_shape=(jax.ShapeDtypeStruct((5, 1024), F32), j...]
where the time goes in v4:
time: 51.3 us; the launch traced here: 51.1 us
  Pallas kernels  50.4 us (98%)
  between operations  0.64 us (1%)
    pallas_call x1, Pallas kernels, on_device(): pl.pallas_call(kernel, out_shape=(jax.ShapeDtypeStruct((5, 1024), F32), j...  49 us
    pallas_call x1, Pallas kernels, on_device(): pl.pallas_call(write_out, out_shape=(jax.ShapeDtypeStruct((5, 1024), F32)...  1.45 us

profile of v4, /device:TPU:1, one launch (start us, length us, event | category | flops | bytes accessed | tf_op | source)
XLA Modules:
  0.0 51.1 jit_solution(18188843879562974208)
XLA Ops:
  0.6 49.0 %shard_map.103 = (f32[5,1024]{1,0:T(8,128)}, f32[3,128]{1,0:T(4,128)}, f32[64,128]{1,0:T(8,128)}) custom-call(f32[5,8192]{1,0:T(8,128)} %design_h.1, f32[64,128]{1,0:T(8,128)} %bitcast.7, f32[64,128]{1,0:T(8,128)} %bitcast.8, f32[64,128]{1,0:T(8,128)} %bitcast.9, f32[3,8192]{1,0:T(4,128)} %ax_h.1, s32[64,128]{1,0:T(8,128)} %bitcast.10, s32[64,128]{1,0:T(8,128)} %bitcast.11, ...), custom_call_target="tpu_custom_call" | custom-call | tf_op jit(solution)/shard_map/pallas_call | solution.py:571
  49.6 1.4 %shard_map.104 = (f32[5,1024]{1,0:T(8,128)}, f32[3,128]{1,0:T(4,128)}, f32[64,128]{1,0:T(8,128)}) custom-call(f32[5,1024]{1,0:T(8,128)} %get-tuple-element.9.params_i, f32[3,128]{1,0:T(4,128)} %get-tuple-element.10.att_i, f32[64,128]{1,0:T(8,128)} %get-tuple-element.11.res_i), custom_call_target="tpu_custom_call" | custom-call | tf_op jit(solution)/shard_map/pallas_call | solution.py:603

commit v5 on v4

--- a/solution.py
+++ b/solution.py
@@ -75,7 +75,7 @@
     params_o, att_o, res_o, out_sem,
     design, obs, wt, ph, ax, sidx, kidx, cnt, in_sem,
     otlo, otk, bb, wl, ax8, acc, mom, momr, par,
-    nloc, nhalf, nsum, nr, npc, nz, nf,
+    nloc, nhalf, nsum, nr, npc, nz, nf, nf2,
     rloc, rhalf, rsum, rr, rpc, rz, cp, cb, resid,
     ma_s, ma_r, pa_s, pa_r, nh_s, nh_r, np_s, np_r, nz_s, nz_r, ng_s, ng_r,
     rh_s, rh_r, rp_s, rp_r, rz_s, rz_r, cg_s, cg_r, from_low, from_high,
@@ -393,16 +393,16 @@
             total = total + nr[i, g]
         npc[g] = total
     heard(last=True)
-    owners = [(16 * g) // 7 for g in range(7)]
-    mine = (7 * z + 15) // 16
-    is_owner = (16 * mine) // 7 == z
-    for g, owner in enumerate(owners):
-        step = (owner + 16 - z) % 16
+    mine, half = z % 8, z // 8
+    is_owner = mine < 7
+    for g in range(7):
+        owner = g + 8 * ((((z + 16 - g) % 16 + 4) // 8) % 2)
+        slot = (z + 20 - owner) % 16
 
         @pl.when(owner != z)
-        def _(g=g, owner=owner, step=step):
+        def _(g=g, owner=owner, slot=slot):
             pltpu.make_async_remote_copy(
-                src_ref=npc.at[g], dst_ref=nz.at[step - 1], send_sem=nz_s, recv_sem=nz_r,
+                src_ref=npc.at[g], dst_ref=nz.at[slot], send_sem=nz_s, recv_sem=nz_r,
                 device_id=(owner * 4 + y, ccd), device_id_type=MESH,
             ).start()
 
@@ -422,13 +422,13 @@
     @pl.when(is_owner)
     def _():
         total = npc[mine]
-        settle(nz, nz_r)
-        for k in range(15):
+        settle(nz.at[0:7], nz_r)
+        for k in (0, 1, 2, 3, 5, 6, 7):
             total = total + nz[k]
-        nf[mine] = total
+        nf2[7 * half + mine] = total
         for k in zsteps:
             pltpu.make_async_remote_copy(
-                src_ref=nf.at[mine], dst_ref=nf.at[mine], send_sem=ng_s, recv_sem=ng_r,
+                src_ref=nf2.at[7 * half + mine], dst_ref=nf2.at[7 * half + mine], send_sem=ng_s, recv_sem=ng_r,
                 device_id=along(k), device_id_type=MESH,
             ).start()
 
@@ -438,11 +438,13 @@
         flat = flat + rz[i]
     @pl.when(is_owner)
     def _():
-        settle(nf.at[0:6], ng_r)
+        settle(nf2.at[0:13], ng_r)
 
     @pl.when(jnp.logical_not(is_owner))
     def _():
-        settle(nf, ng_r)
+        settle(nf2, ng_r)
+
+    nf[...] = nf2[0:7] + nf2[7:14]
 
     def wide(pieces):
         return jnp.concatenate([jnp.broadcast_to(piece, (8, 128)) for piece in pieces], 1)
@@ -541,7 +543,7 @@
     @pl.when(is_owner)
     def _():
         settle(nz.at[0:6], nz_s)
-        settle(nz, ng_s)
+        settle(rz, ng_s)
 
     @pl.when(jnp.logical_not(is_owner))
     def _():
@@ -586,7 +588,7 @@
             vm(14, 64, 128), vm(64, 128), vm(8, 8192),
             vm(256, 256), vm(8, 24, 128), vm(7, 24, 128), vm(8, 8, 128),
             vm(TILES, 24, 128), vm(HALF, 24, 128), vm(16, 7, 8, 128), vm(15, 7, 8, 128),
-            vm(7, 8, 128), vm(15, 8, 128), vm(7, 8, 128),
+            vm(7, 8, 128), vm(8, 8, 128), vm(7, 8, 128), vm(14, 8, 128),
             vm(TILES, 4, 128), vm(HALF, 4, 128), vm(16, 3, 4, 128), vm(15, 3, 4, 128),
             vm(8, 128), vm(15, 8, 128), vm(2, 4, 128), vm(TILES, 4, 128), vm(64, 128),
         ]

time: 51.3 us -> 50.4 us (0.982)
  Pallas kernels: 50.4 us -> 49.6 us
    pallas_call x1, Pallas kernels: 49 us -> 48.1 us  [on_device(): pl.pallas_call(kernel, out_shape=(jax.ShapeDtypeStruct((5, 1024), F32), j...]
where the time goes in v5:
time: 50.4 us; the launch traced here: 50.2 us
  Pallas kernels  49.6 us (98%)
  between operations  0.64 us (1%)
    pallas_call x1, Pallas kernels, on_device(): pl.pallas_call(kernel, out_shape=(jax.ShapeDtypeStruct((5, 1024), F32), j...  48.1 us
    pallas_call x1, Pallas kernels, on_device(): pl.pallas_call(write_out, out_shape=(jax.ShapeDtypeStruct((5, 1024), F32)...  1.45 us

profile of v5, /device:TPU:1, one launch (start us, length us, event | category | flops | bytes accessed | tf_op | source)
XLA Modules:
  0.0 50.2 jit_solution(9924525446617739785)
XLA Ops:
  0.6 48.1 %shard_map.103 = (f32[5,1024]{1,0:T(8,128)}, f32[3,128]{1,0:T(4,128)}, f32[64,128]{1,0:T(8,128)}) custom-call(f32[5,8192]{1,0:T(8,128)} %design_h.1, f32[64,128]{1,0:T(8,128)} %bitcast.7, f32[64,128]{1,0:T(8,128)} %bitcast.8, f32[64,128]{1,0:T(8,128)} %bitcast.9, f32[3,8192]{1,0:T(4,128)} %ax_h.1, s32[64,128]{1,0:T(8,128)} %bitcast.10, s32[64,128]{1,0:T(8,128)} %bitcast.11, ...), custom_call_target="tpu_custom_call" | custom-call | tf_op jit(solution)/shard_map/pallas_call | solution.py:573
  48.8 1.4 %shard_map.104 = (f32[5,1024]{1,0:T(8,128)}, f32[3,128]{1,0:T(4,128)}, f32[64,128]{1,0:T(8,128)}) custom-call(f32[5,1024]{1,0:T(8,128)} %get-tuple-element.9.params_i, f32[3,128]{1,0:T(4,128)} %get-tuple-element.10.att_i, f32[64,128]{1,0:T(8,128)} %get-tuple-element.11.res_i), custom_call_target="tpu_custom_call" | custom-call | tf_op jit(solution)/shard_map/pallas_call | solution.py:605

commit v6 on v5

--- a/solution.py
+++ b/solution.py
@@ -316,6 +316,7 @@
 
     for i in range(15):
         to_owner(i)
+    heard()
     heard()
 
     settle(par.at[0:7], pa_r)
@@ -385,14 +386,13 @@
         there = ((y + ky) % 4) * 4 + (x + kx) % 4
         send(rsum.at[there], rr.at[i], rp_s, rp_r, plane(ky, kx, 0))
 
-    heard()
+    heard(last=True)
     settle(nr, np_r)
     for g in range(7):
         total = nsum[chip, g]
         for i in range(15):
             total = total + nr[i, g]
         npc[g] = total
-    heard(last=True)
     mine, half = z % 8, z // 8
     is_owner = mine < 7
     for g in range(7):

time: 50.4 us -> 51.1 us (1.014)
  Pallas kernels: 49.6 us -> 50.2 us
    pallas_call x1, Pallas kernels: 48.1 us -> 48.8 us  [on_device(): pl.pallas_call(kernel, out_shape=(jax.ShapeDtypeStruct((5, 1024), F32), j...]
where the time goes in v6:
time: 51.1 us; the launch traced here: 50.9 us
  Pallas kernels  50.2 us (98%)
  between operations  0.64 us (1%)
    pallas_call x1, Pallas kernels, on_device(): pl.pallas_call(kernel, out_shape=(jax.ShapeDtypeStruct((5, 1024), F32), j...  48.8 us
    pallas_call x1, Pallas kernels, on_device(): pl.pallas_call(write_out, out_shape=(jax.ShapeDtypeStruct((5, 1024), F32)...  1.45 us

profile of v6, /device:TPU:1, one launch (start us, length us, event | category | flops | bytes accessed | tf_op | source)
XLA Modules:
  0.0 50.9 jit_solution(17090831233616084331)
XLA Ops:
  0.6 48.8 %shard_map.103 = (f32[5,1024]{1,0:T(8,128)}, f32[3,128]{1,0:T(4,128)}, f32[64,128]{1,0:T(8,128)}) custom-call(f32[5,8192]{1,0:T(8,128)} %design_h.1, f32[64,128]{1,0:T(8,128)} %bitcast.7, f32[64,128]{1,0:T(8,128)} %bitcast.8, f32[64,128]{1,0:T(8,128)} %bitcast.9, f32[3,8192]{1,0:T(4,128)} %ax_h.1, s32[64,128]{1,0:T(8,128)} %bitcast.10, s32[64,128]{1,0:T(8,128)} %bitcast.11, ...), custom_call_target="tpu_custom_call" | custom-call | tf_op jit(solution)/shard_map/pallas_call | solution.py:573
  49.4 1.4 %shard_map.104 = (f32[5,1024]{1,0:T(8,128)}, f32[3,128]{1,0:T(4,128)}, f32[64,128]{1,0:T(8,128)}) custom-call(f32[5,1024]{1,0:T(8,128)} %get-tuple-element.9.params_i, f32[3,128]{1,0:T(4,128)} %get-tuple-element.10.att_i, f32[64,128]{1,0:T(8,128)} %get-tuple-element.11.res_i), custom_call_target="tpu_custom_call" | custom-call | tf_op jit(solution)/shard_map/pallas_call | solution.py:605
